TPU v7x, 128 devices: a whole 4x4x4 slice. The times are simulated.
128 devices in a mesh: section: 4 (over x), dom: 32 (over z, y, core).
Axes of the slice: x: 4, y: 4, z: 4, core: 2. Of those that a mesh axis runs over, the one named last changes fastest.
Arguments:
- measures: bfloat16 [524288, 128], P(('section', 'dom')), may hold values from -6 to 6
- pred_columns: int32 [2, 524288], P(None, ('section', 'dom')), may hold values from 0 to 99
- bounds: int32 [2, 2], replicated, may hold values from 0 to 100
- lengths: int32 [4096], P(('section', 'dom')), may hold values from 120 to 128
- destination: int32 [524288, 1], P(('section', 'dom')), may hold values from 0 to 127; in each aligned block of 4096 rows (0 to 4095, 4096 to 8191, ...) at most 64 rows name the same one
- key_offset: int32 [524288], P(('section', 'dom')), may hold values from 0 to 2047
- group_ids: int32 [524288], P(('section', 'dom')), may hold values from 0 to 4095
- build_table: bfloat16 [262144, 128], P(('section', 'dom')), may hold values from -6 to 6
Outputs:
- group_sums: float32 [4096, 128], P(('section', 'dom'))
- top_scores: float32 [16], replicated
Inputs may be any that keep to these rules, and one draw needn't show every extreme that they name: Among the rows of one device, no destination is named more than 64 times, a bound that some block reaches.
All inputs are finite; a program needn't handle non-finite values.
Results may differ from a plain program's by a relative error of at most 0.0048.
Values may be sent and summed in bfloat16 or wider, within the bound.
No kernel may reach another device: no remote copies, remote signals or barrier semaphores. Data moves between devices by JAX's collectives and lax.ppermute only.
A program may use at most 64 MiB of HBM per device.

v0:
```python
import jax
import jax.numpy as jnp
from jax import lax
from jax.sharding import Mesh
from jax.sharding import PartitionSpec as P

BLOCK = 128
TOPK = 16
GRP_DEV = 32
SECTION_DOM = ("section", "dom_0", "dom_1", "dom_2")


def sent_together(arrays, axis, split_dim, concat_dim, along):
    ends, at = ([], 0)
    for a in arrays[:-1]:
        at += a.shape[along]
        ends.append(at)
    both = jnp.concatenate(arrays, axis=along)
    return tuple(
        jnp.split(
            lax.all_to_all(both, axis, split_axis=split_dim, concat_axis=concat_dim, tiled=True),
            ends,
            axis=along,
        )
    )


def in_blocks(value, dim, devices):
    before, after = (value.shape[:dim], value.shape[dim + 1 :])
    return jnp.moveaxis(value.reshape(*before, devices, -1, *after), dim, 0)


def sent_and_summed(value, axis, dim):
    devices = lax.axis_size(axis)
    blocks = lax.all_to_all(in_blocks(value, dim, devices), axis, 0, 0, tiled=True)
    return jnp.sum(blocks.astype(jnp.float32), axis=0)


def sum_by_axis(value, axes, dim):
    far, near = axes
    blocks = in_blocks(value, dim, lax.axis_size(far))
    nearer = sent_and_summed(blocks, near, dim + 1)
    arrived = lax.all_to_all(
        nearer.astype(jnp.bfloat16), far, split_axis=0, concat_axis=0, tiled=True
    )
    return arrived.astype(jnp.float32).sum(axis=0)


def copy_for_each(value, axis):
    copies = jnp.broadcast_to(value, (lax.axis_size(axis), *value.shape))
    return lax.all_to_all(copies, axis, split_axis=0, concat_axis=0, tiled=True)


def in_order(blocks, dim):
    lengths = list(blocks.shape[1:])
    lengths[dim] *= blocks.shape[0]
    return jnp.moveaxis(blocks, 0, dim).reshape(lengths)


def gathered_by_axis(value, axes, dim):
    far, near = axes
    blocks = copy_for_each(copy_for_each(value, far), near)
    return in_order(blocks.swapaxes(0, 1).reshape(-1, *value.shape), dim)


def slot_positions(targets, count_targets):
    matches = (targets[:, None] == jnp.arange(count_targets, dtype=jnp.int32)[None, :]).astype(
        jnp.int32
    )
    before = jnp.cumsum(matches, axis=0) - 1
    return jnp.sum(before * matches, axis=1)


def fill_slots(places, total_slots, payload, first_ints, second_ints):
    payload_buffer = (
        jnp.zeros((total_slots, payload.shape[1]), payload.dtype).at[places].set(payload)
    )
    first_buffer = jnp.zeros((total_slots,), jnp.int32).at[places].set(first_ints)
    second_buffer = jnp.zeros((total_slots,), jnp.int32).at[places].set(second_ints)
    return (payload_buffer, first_buffer, second_buffer)


def join_owned(received, local_keys, build_table, block_rows):
    feat_width = received.shape[1]
    blocks_payload = received.reshape(-1, block_rows, feat_width)
    blocks_keys = local_keys.reshape(-1, block_rows)

    def one_block(members):
        payload_part, keys_part = members
        picker = (
            keys_part[:, None] == jnp.arange(build_table.shape[0], dtype=jnp.int32)[None, :]
        ).astype(jnp.bfloat16)
        fetched = jnp.dot(picker, build_table, preferred_element_type=jnp.float32)
        return (payload_part.astype(jnp.float32) * fetched).astype(jnp.bfloat16)

    joined = lax.map(one_block, (blocks_payload, blocks_keys))
    return joined.reshape(received.shape)


def group_terms(joined, received_groups, count, block_rows):
    feat_width = joined.shape[1]
    blocks_joined = joined.reshape(-1, block_rows, feat_width)
    blocks_groups = received_groups.reshape(-1, block_rows)
    labels = jnp.arange(count, dtype=jnp.int32)

    def add_block(running, members):
        joined_part, group_part = members
        picker = (labels[:, None] == group_part[None, :]).astype(jnp.bfloat16)
        return (running + jnp.dot(picker, joined_part, preferred_element_type=jnp.float32), None)

    running, unused = lax.scan(
        add_block, jnp.zeros((count, feat_width), jnp.float32), (blocks_joined, blocks_groups)
    )
    return running


def on_device(
    measures, pred_columns, bounds, lengths, destination, key_offset, group_ids, build_table
):
    row_count = measures.shape[0]
    feat_width = measures.shape[1]
    devices = lax.axis_size(SECTION_DOM)
    within = (lengths[:, None] > jnp.arange(BLOCK, dtype=jnp.int32)[None, :]).reshape(row_count)
    passes = jnp.all((pred_columns >= bounds[:, 0:1]) & (pred_columns < bounds[:, 1:2]), axis=0)
    usable = within & passes
    payload = jnp.where(usable[:, None], measures, jnp.zeros_like(measures))
    targets = destination[:, 0]
    capacity = 2 * row_count // devices
    total_slots = devices * capacity
    places = targets * capacity + slot_positions(targets, devices)
    buffers = fill_slots(places, total_slots, payload, key_offset, group_ids)
    shaped = (
        buffers[0].reshape(devices, capacity, feat_width),
        buffers[1].reshape(devices, capacity),
        buffers[2].reshape(devices, capacity),
    )
    arrived = (
        lax.all_to_all(shaped[0], SECTION_DOM, split_axis=0, concat_axis=0, tiled=True),
        *sent_together((shaped[1], shaped[2]), SECTION_DOM, 0, 0, 1),
    )
    received = arrived[0].reshape(total_slots, feat_width)
    received_keys = arrived[1].reshape(total_slots)
    received_groups = arrived[2].reshape(total_slots)
    block_rows = 1024
    joined = join_owned(received, received_keys, build_table, block_rows)
    group_sums = sum_by_axis(
        group_terms(
            joined, received_groups, GRP_DEV * lax.axis_size(SECTION_DOM), block_rows
        ).astype(jnp.bfloat16),
        (("section", "dom_0", "dom_1"), "dom_2"),
        0,
    )
    scores = jnp.mean(group_sums, axis=1)
    everything = gathered_by_axis(scores, (("section", "dom_0", "dom_1"), "dom_2"), 0)
    leaders = lax.top_k(everything, TOPK)[0]
    return (group_sums, leaders)


def solution(mesh):
    finer = Mesh(
        mesh.devices.reshape(mesh.shape["section"], 4, 4, 2), ("section", "dom_0", "dom_1", "dom_2")
    )
    return jax.shard_map(
        on_device,
        mesh=finer,
        in_specs=(
            P(SECTION_DOM, None),
            P(None, SECTION_DOM),
            P(),
            P(SECTION_DOM),
            P(SECTION_DOM, None),
            P(SECTION_DOM),
            P(SECTION_DOM),
            P(SECTION_DOM, None),
        ),
        out_specs=(P(SECTION_DOM, None), P()),
        check_vma=False,
    )
```

profile of v0, /device:TPU:1, one launch (start us, length us, event | category | flops | bytes accessed | tf_op | source)
XLA Modules:
  0.0 216.2 jit_solution(15365105273221402284)
XLA Ops:
  0.6 0.8 copy.24
  1.4 0.6 fusion.15
  2.1 0.3 add_add_fusion
  2.4 1.2 copy.25
  3.7 1.4 fusion.14
  5.2 15.7 %scatter_custom_fusion.1 = s32[8192]{0:T(1024)S(1)} fusion(s32[4096]{0:T(1024)S(1)} %bitcast.68, s32[4096]{0:T(1024)} %param.18, s32[]{:T(128)} %constant.45.clone.1), kind=kCustom, calls=%fused_computation.40 | custom fusion | bytes 33280 | tf_op jit(solution)/shard_map/scatter | solution.py:79
  21.0 15.7 %scatter_custom_fusion = s32[8192]{0:T(1024)S(1)} fusion(s32[4096]{0:T(1024)S(1)} %bitcast.69, s32[4096]{0:T(1024)} %param.17, s32[]{:T(128)} %constant.45.clone.1), kind=kCustom, calls=%fused_computation.42 | custom fusion | bytes 33280 | tf_op jit(solution)/shard_map/scatter | solution.py:78
  36.8 0.7 pad_add_fusion
  37.5 11.5 %all-to-all-start = ((s32[128,1,128]{2,1,0:T(1,128)}), s32[128,1,128]{2,1,0:T(1,128)S(1)}, u32[]{:S(2)}, u32[]{:S(2)}) async-start(s32[128,1,128]{2,1,0:T(1,128)} %bitcast.11), calls=%async_computation | async-start | bytes 131072 | tf_op jit(solution)/shard_map/all_to_all | solution.py:21
  49.0 0.2 slice_reduce_fusion.1
  49.2 0.1 and_reduce_fusion
  49.4 14.6 %scatter_custom_fusion.2 = bf16[8192,128]{1,0:T(8,128)(2,1)} fusion(s32[4096]{0:T(1024)S(1)} %bitcast.70, bf16[4096,128]{1,0:T(8,128)(2,1)S(1)} %copy-done, bf16[]{:T(256)} %constant.47.clone.1, pred[4096]{0:T(1024)(128)(4,1)S(1)} %fusion.28), kind=kCustom, calls=%fused_computation.29 | custom fusion | flops 524288 | bytes 3150848 | tf_op jit(solution)/shard_map/scatter | solution.py:76
  64.0 10.2 %all-to-all-start.1 = ((bf16[128,64,128]{2,1,0:T(8,128)(2,1)}), bf16[128,64,128]{2,1,0:T(8,128)(2,1)}, u32[]{:S(2)}, u32[]{:S(2)}) async-start(bf16[128,64,128]{2,1,0:T(8,128)(2,1)} %bitcast.14), calls=%async_computation.1 | async-start | bytes 4194304 | tf_op jit(solution)/shard_map/all_to_all | solution.py:138
  74.4 0.1 reshape_reshape.17
  74.5 29.6 %all-to-all-done.1 = bf16[128,64,128]{2,1,0:T(8,128)(2,1)} async-done(((bf16[128,64,128]{2,1,0:T(8,128)(2,1)}), bf16[128,64,128]{2,1,0:T(8,128)(2,1)}, u32[]{:S(2)}, u32[]{:S(2)}) %all-to-all-start.1) | async-done | bytes 2097184 | tf_op jit(solution)/shard_map/all_to_all | solution.py:138
  104.1 25.4 %while.21 = (s32[]{:T(128)}, bf16[8,1024,128]{2,1,0:T(8,128)(2,1)}, bf16[8,1024,128]{2,1,0:T(8,128)(2,1)}, s32[8,1024]{1,0:T(8,128)S(1)}, bf16[2048,128]{1,0:T(8,128)(2,1)S(1)}, /*index=5*/s32[]{:T(128)}) while((s32[]{:T(128)}, bf16[8,1024,128]{2,1,0:T(8,128)(2,1)}, bf16[8,1024,128]{2,1,0:T(8,128)(2,1)}, s32[8,1024]{1,0:T(8,128)S(1)}, ...), condition=%wide.region_8.9_spmd, body=%wide.region_7.8_spmd.sunk | while | flops 539361280 | bytes 1060949 | solution.py:96
  104.1 3.1 %fusion.36 = bf16[8,1024,128]{2,1,0:T(8,128)(2,1)} fusion(bf16[8,1024,128]{2,1,0:T(8,128)(2,1)} %get-tuple-element.165, s32[]{:T(128)S(6)} %copy.33, bf16[2048,128]{1,0:T(8,128)(2,1)S(1)} %get-tuple-element.174, s32[1024]{0:T(1024)S(1)} %bitcast.66, bf16[8,1024,128]{2,1,0:T(8,128)(2,1)} %get-tuple-element.172), kind=kOutput, calls=%fused_computation.10.clone.1 | convolution fusion | flops 539361280 | bytes 1052676 | tf_op jit(solution)/shard_map/while/body/eval_jaxpr/dot_general | solution.py:93
  107.3 3.2 %fusion.36 = bf16[8,1024,128]{2,1,0:T(8,128)(2,1)} fusion(bf16[8,1024,128]{2,1,0:T(8,128)(2,1)} %get-tuple-element.165, s32[]{:T(128)S(6)} %copy.33, bf16[2048,128]{1,0:T(8,128)(2,1)S(1)} %get-tuple-element.174, s32[1024]{0:T(1024)S(1)} %bitcast.66, bf16[8,1024,128]{2,1,0:T(8,128)(2,1)} %get-tuple-element.172), kind=kOutput, calls=%fused_computation.10.clone.1 | convolution fusion | flops 539361280 | bytes 1052676 | tf_op jit(solution)/shard_map/while/body/eval_jaxpr/dot_general | solution.py:93
  110.4 3.2 %fusion.36 = bf16[8,1024,128]{2,1,0:T(8,128)(2,1)} fusion(bf16[8,1024,128]{2,1,0:T(8,128)(2,1)} %get-tuple-element.165, s32[]{:T(128)S(6)} %copy.33, bf16[2048,128]{1,0:T(8,128)(2,1)S(1)} %get-tuple-element.174, s32[1024]{0:T(1024)S(1)} %bitcast.66, bf16[8,1024,128]{2,1,0:T(8,128)(2,1)} %get-tuple-element.172), kind=kOutput, calls=%fused_computation.10.clone.1 | convolution fusion | flops 539361280 | bytes 1052676 | tf_op jit(solution)/shard_map/while/body/eval_jaxpr/dot_general | solution.py:93
  113.6 3.2 %fusion.36 = bf16[8,1024,128]{2,1,0:T(8,128)(2,1)} fusion(bf16[8,1024,128]{2,1,0:T(8,128)(2,1)} %get-tuple-element.165, s32[]{:T(128)S(6)} %copy.33, bf16[2048,128]{1,0:T(8,128)(2,1)S(1)} %get-tuple-element.174, s32[1024]{0:T(1024)S(1)} %bitcast.66, bf16[8,1024,128]{2,1,0:T(8,128)(2,1)} %get-tuple-element.172), kind=kOutput, calls=%fused_computation.10.clone.1 | convolution fusion | flops 539361280 | bytes 1052676 | tf_op jit(solution)/shard_map/while/body/eval_jaxpr/dot_general | solution.py:93
  116.8 3.2 %fusion.36 = bf16[8,1024,128]{2,1,0:T(8,128)(2,1)} fusion(bf16[8,1024,128]{2,1,0:T(8,128)(2,1)} %get-tuple-element.165, s32[]{:T(128)S(6)} %copy.33, bf16[2048,128]{1,0:T(8,128)(2,1)S(1)} %get-tuple-element.174, s32[1024]{0:T(1024)S(1)} %bitcast.66, bf16[8,1024,128]{2,1,0:T(8,128)(2,1)} %get-tuple-element.172), kind=kOutput, calls=%fused_computation.10.clone.1 | convolution fusion | flops 539361280 | bytes 1052676 | tf_op jit(solution)/shard_map/while/body/eval_jaxpr/dot_general | solution.py:93
  120.0 3.2 %fusion.36 = bf16[8,1024,128]{2,1,0:T(8,128)(2,1)} fusion(bf16[8,1024,128]{2,1,0:T(8,128)(2,1)} %get-tuple-element.165, s32[]{:T(128)S(6)} %copy.33, bf16[2048,128]{1,0:T(8,128)(2,1)S(1)} %get-tuple-element.174, s32[1024]{0:T(1024)S(1)} %bitcast.66, bf16[8,1024,128]{2,1,0:T(8,128)(2,1)} %get-tuple-element.172), kind=kOutput, calls=%fused_computation.10.clone.1 | convolution fusion | flops 539361280 | bytes 1052676 | tf_op jit(solution)/shard_map/while/body/eval_jaxpr/dot_general | solution.py:93
  123.1 3.2 %fusion.36 = bf16[8,1024,128]{2,1,0:T(8,128)(2,1)} fusion(bf16[8,1024,128]{2,1,0:T(8,128)(2,1)} %get-tuple-element.165, s32[]{:T(128)S(6)} %copy.33, bf16[2048,128]{1,0:T(8,128)(2,1)S(1)} %get-tuple-element.174, s32[1024]{0:T(1024)S(1)} %bitcast.66, bf16[8,1024,128]{2,1,0:T(8,128)(2,1)} %get-tuple-element.172), kind=kOutput, calls=%fused_computation.10.clone.1 | convolution fusion | flops 539361280 | bytes 1052676 | tf_op jit(solution)/shard_map/while/body/eval_jaxpr/dot_general | solution.py:93
  126.3 3.2 %fusion.36 = bf16[8,1024,128]{2,1,0:T(8,128)(2,1)} fusion(bf16[8,1024,128]{2,1,0:T(8,128)(2,1)} %get-tuple-element.165, s32[]{:T(128)S(6)} %copy.33, bf16[2048,128]{1,0:T(8,128)(2,1)S(1)} %get-tuple-element.174, s32[1024]{0:T(1024)S(1)} %bitcast.66, bf16[8,1024,128]{2,1,0:T(8,128)(2,1)} %get-tuple-element.172), kind=kOutput, calls=%fused_computation.10.clone.1 | convolution fusion | flops 539361280 | bytes 1052676 | tf_op jit(solution)/shard_map/while/body/eval_jaxpr/dot_general | solution.py:93
  129.5 35.8 %while.22 = (s32[]{:T(128)}, f32[4096,128]{1,0:T(8,128)S(1)}, s32[8,1024]{1,0:T(8,128)S(1)}, bf16[8,1024,128]{2,1,0:T(8,128)(2,1)}, s32[]{:T(128)}, /*index=5*/s32[]{:T(128)}) while((s32[]{:T(128)}, f32[4096,128]{1,0:T(8,128)S(1)}, s32[8,1024]{1,0:T(8,128)S(1)}, bf16[8,1024,128]{2,1,0:T(8,128)(2,1)}, s32[]{:T(128)}, ...), condition=%wide.region_10.11_spmd.clone, body=%wide.region_9.10_spmd.clone.sunk | while | flops 1078984704 | bytes 4468831 | solution.py:111
  129.5 4.4 %fusion.38 = f32[4096,128]{1,0:T(8,128)S(1)} fusion(s32[1024]{0:T(1024)S(1)} %bitcast.65, f32[4096,128]{1,0:T(8,128)S(1)} %get-tuple-element.183, pred[]{:T(512)S(6)} %compare.21, bf16[8,1024,128]{2,1,0:T(8,128)(2,1)} %get-tuple-element.191, s32[]{:T(128)S(6)} %copy.39), kind=kOutput, calls=%fused_computation.15.clone.1 | convolution fusion | flops 1078984704 | bytes 4460549 | tf_op jit(solution)/shard_map/while/body/eval_jaxpr/dot_general | solution.py:109
  134.0 4.4 %fusion.38 = f32[4096,128]{1,0:T(8,128)S(1)} fusion(s32[1024]{0:T(1024)S(1)} %bitcast.65, f32[4096,128]{1,0:T(8,128)S(1)} %get-tuple-element.183, pred[]{:T(512)S(6)} %compare.21, bf16[8,1024,128]{2,1,0:T(8,128)(2,1)} %get-tuple-element.191, s32[]{:T(128)S(6)} %copy.39), kind=kOutput, calls=%fused_computation.15.clone.1 | convolution fusion | flops 1078984704 | bytes 4460549 | tf_op jit(solution)/shard_map/while/body/eval_jaxpr/dot_general | solution.py:109
  138.5 4.4 %fusion.38 = f32[4096,128]{1,0:T(8,128)S(1)} fusion(s32[1024]{0:T(1024)S(1)} %bitcast.65, f32[4096,128]{1,0:T(8,128)S(1)} %get-tuple-element.183, pred[]{:T(512)S(6)} %compare.21, bf16[8,1024,128]{2,1,0:T(8,128)(2,1)} %get-tuple-element.191, s32[]{:T(128)S(6)} %copy.39), kind=kOutput, calls=%fused_computation.15.clone.1 | convolution fusion | flops 1078984704 | bytes 4460549 | tf_op jit(solution)/shard_map/while/body/eval_jaxpr/dot_general | solution.py:109
  142.9 4.4 %fusion.38 = f32[4096,128]{1,0:T(8,128)S(1)} fusion(s32[1024]{0:T(1024)S(1)} %bitcast.65, f32[4096,128]{1,0:T(8,128)S(1)} %get-tuple-element.183, pred[]{:T(512)S(6)} %compare.21, bf16[8,1024,128]{2,1,0:T(8,128)(2,1)} %get-tuple-element.191, s32[]{:T(128)S(6)} %copy.39), kind=kOutput, calls=%fused_computation.15.clone.1 | convolution fusion | flops 1078984704 | bytes 4460549 | tf_op jit(solution)/shard_map/while/body/eval_jaxpr/dot_general | solution.py:109
  147.4 4.4 %fusion.38 = f32[4096,128]{1,0:T(8,128)S(1)} fusion(s32[1024]{0:T(1024)S(1)} %bitcast.65, f32[4096,128]{1,0:T(8,128)S(1)} %get-tuple-element.183, pred[]{:T(512)S(6)} %compare.21, bf16[8,1024,128]{2,1,0:T(8,128)(2,1)} %get-tuple-element.191, s32[]{:T(128)S(6)} %copy.39), kind=kOutput, calls=%fused_computation.15.clone.1 | convolution fusion | flops 1078984704 | bytes 4460549 | tf_op jit(solution)/shard_map/while/body/eval_jaxpr/dot_general | solution.py:109
  151.9 4.4 %fusion.38 = f32[4096,128]{1,0:T(8,128)S(1)} fusion(s32[1024]{0:T(1024)S(1)} %bitcast.65, f32[4096,128]{1,0:T(8,128)S(1)} %get-tuple-element.183, pred[]{:T(512)S(6)} %compare.21, bf16[8,1024,128]{2,1,0:T(8,128)(2,1)} %get-tuple-element.191, s32[]{:T(128)S(6)} %copy.39), kind=kOutput, calls=%fused_computation.15.clone.1 | convolution fusion | flops 1078984704 | bytes 4460549 | tf_op jit(solution)/shard_map/while/body/eval_jaxpr/dot_general | solution.py:109
  156.4 4.4 %fusion.38 = f32[4096,128]{1,0:T(8,128)S(1)} fusion(s32[1024]{0:T(1024)S(1)} %bitcast.65, f32[4096,128]{1,0:T(8,128)S(1)} %get-tuple-element.183, pred[]{:T(512)S(6)} %compare.21, bf16[8,1024,128]{2,1,0:T(8,128)(2,1)} %get-tuple-element.191, s32[]{:T(128)S(6)} %copy.39), kind=kOutput, calls=%fused_computation.15.clone.1 | convolution fusion | flops 1078984704 | bytes 4460549 | tf_op jit(solution)/shard_map/while/body/eval_jaxpr/dot_general | solution.py:109
  160.8 4.4 %fusion.38 = f32[4096,128]{1,0:T(8,128)S(1)} fusion(s32[1024]{0:T(1024)S(1)} %bitcast.65, f32[4096,128]{1,0:T(8,128)S(1)} %get-tuple-element.183, pred[]{:T(512)S(6)} %compare.21, bf16[8,1024,128]{2,1,0:T(8,128)(2,1)} %get-tuple-element.191, s32[]{:T(128)S(6)} %copy.39), kind=kOutput, calls=%fused_computation.15.clone.1 | convolution fusion | flops 1078984704 | bytes 4460549 | tf_op jit(solution)/shard_map/while/body/eval_jaxpr/dot_general | solution.py:109
  165.3 0.1 convert_element_type.25
  165.5 5.5 %all_to_all.41 = bf16[2,64,32,128]{3,2,1,0:T(8,128)(2,1)S(1)} all-to-all(bf16[2,64,32,128]{3,2,1,0:T(8,128)(2,1)S(1)} %copy.27), channel_id=1, replica_groups=mesh['section'=4,'dom_0'=4,'dom_1'=4,'dom_2'=2] {'dom_2'}, dimensions={0} | all-to-all | bytes 2097152 | tf_op jit(solution)/shard_map/all_to_all | solution.py:35
  170.9 0.5 reduce_sum.43
  171.4 16.3 %all_to_all.42 = bf16[64,32,128]{2,1,0:T(8,128)(2,1)S(1)} all-to-all(bf16[64,32,128]{2,1,0:T(8,128)(2,1)S(1)} %reduce_sum.43), channel_id=1, replica_groups=mesh['section'=4,'dom_0'=4,'dom_1'=4,'dom_2'=2] {'section','dom_0','dom_1'}, dimensions={0} | all-to-all | bytes 1048576 | tf_op jit(solution)/shard_map/all_to_all | solution.py:43
  187.7 0.7 convert_reduce_fusion
  188.4 13.2 %all_to_all.43 = f32[64,1,32]{2,1,0:T(1,128)S(1)} all-to-all(f32[64,1,32]{2,1,0:T(1,128)S(1)} %broadcast_in_dim.46), channel_id=1, replica_groups=mesh['section'=4,'dom_0'=4,'dom_1'=4,'dom_2'=2] {'section','dom_0','dom_1'}, dimensions={0} | all-to-all | bytes 16384 | tf_op jit(solution)/shard_map/all_to_all | solution.py:51
  201.7 0.1 reshape.97
  201.8 6.6 %all_to_all.44 = f32[2,1,2048]{2,1,0:T(1,128)S(1)} all-to-all(f32[2,1,2048]{2,1,0:T(1,128)S(1)} %reshape.97), channel_id=1, replica_groups=mesh['section'=4,'dom_0'=4,'dom_1'=4,'dom_2'=2] {'dom_2'}, dimensions={0} | all-to-all | bytes 32768 | tf_op jit(solution)/shard_map/all_to_all | solution.py:51
  208.3 0.5 broadcast.67
  208.8 0.7 reduce.6
  209.5 0.1 reshape.98
  209.6 0.1 copy.29
  209.7 0.1 reshape_reshape.19
  209.9 5.9 %top_k.9 = (f32[4096]{0:T(1024)S(1)}, s32[4096]{0:T(1024)}) sort(f32[4096]{0:T(1024)S(1)} %reshape_reshape.19, s32[4096]{0:T(1024)S(1)} %iota.21), dimensions={0}, to_apply=%region_14.15 | sort | flops 49152 | bytes 65536 | tf_op jit(solution)/shard_map/top_k | solution.py:155
  215.7 0.5 top_k.10
  (47 shorter events, 0.8 us)
Async XLA Ops:
  2.4 1.3 copy-start.1
  3.6 45.3 %copy-start.3 = (s32[2,2]{1,0:T(2,128)S(1)}, s32[2,2]{1,0:T(2,128)}, u32[]{:S(2)}) copy-start(s32[2,2]{1,0:T(2,128)} %param.14) | copy-start | bytes 52
  3.6 45.5 %copy-start.2 = (s32[2,4096]{1,0:T(2,128)S(1)}, s32[2,4096]{1,0:T(2,128)}, u32[]{:S(2)}) copy-start(s32[2,4096]{1,0:T(2,128)} %param.13) | copy-start | bytes 98308
  3.7 45.7 %copy-start.4 = (s32[32]{0:T(128)S(1)}, s32[32]{0:T(128)}, u32[]{:S(2)}) copy-start(s32[32]{0:T(128)} %param.15) | copy-start | bytes 388
  3.7 45.7 %copy-start = (bf16[4096,128]{1,0:T(8,128)(2,1)S(1)}, bf16[4096,128]{1,0:T(8,128)(2,1)}, u32[]{:S(2)}) copy-start(bf16[4096,128]{1,0:T(8,128)(2,1)} %param.12) | copy-start | bytes 3145732
  37.5 26.5 %all-to-all-start = ((s32[128,1,128]{2,1,0:T(1,128)}), s32[128,1,128]{2,1,0:T(1,128)S(1)}, u32[]{:S(2)}, u32[]{:S(2)}) async-start(s32[128,1,128]{2,1,0:T(1,128)} %bitcast.11), calls=%async_computation | async-start | bytes 131072 | tf_op jit(solution)/shard_map/all_to_all | solution.py:21
  64.0 40.1 %copy-start.5 = (bf16[2048,128]{1,0:T(8,128)(2,1)S(1)}, bf16[2048,128]{1,0:T(8,128)(2,1)}, u32[]{:S(2)}) copy-start(bf16[2048,128]{1,0:T(8,128)(2,1)} %param.19) | copy-start | bytes 1572868
  64.0 40.1 %all-to-all-start.1 = ((bf16[128,64,128]{2,1,0:T(8,128)(2,1)}), bf16[128,64,128]{2,1,0:T(8,128)(2,1)}, u32[]{:S(2)}, u32[]{:S(2)}) async-start(bf16[128,64,128]{2,1,0:T(8,128)(2,1)} %bitcast.14), calls=%async_computation.1 | async-start | bytes 4194304 | tf_op jit(solution)/shard_map/all_to_all | solution.py:138
where the time goes:
time: 217 us; the launch traced here: 216 us
  matrix products  60.8 us (28%)
  blocking collectives  41.5 us (19%)
  local copies, waits for them, and re-layouts  35.8 us (16%)
  waiting for transfers between devices  29.6 us (14%)
  other arithmetic  25.8 us (12%)
  starting transfers between devices  21.7 us (10%)
    dot_general x8, matrix products, add_block(): jnp.dot(picker, joined_part, preferred_element_type=jnp.float32)  35.5 us
    all_to_all x1, waiting for transfers between devices, on_device(): lax.all_to_all(shaped[0], SECTION_DOM, split_axis=0, concat_axis=0, tiled...  29.6 us
    dot_general x8, matrix products, one_block(): fetched = jnp.dot(picker, build_table, preferred_element_type=jnp.float32)  25.3 us
    all_to_all x2, blocking collectives, copy_for_each(): return lax.all_to_all(copies, axis, split_axis=0, concat_axis=0, tiled=True)  19.7 us
    all_to_all x1, blocking collectives, sum_by_axis(): lax.all_to_all(nearer.astype(jnp.bfloat16), far, split_axis=0, concat_axi...  16.3 us
    scatter x1, local copies, waits for them, and re-layouts, fill_slots(): jnp.zeros((total_slots,), jnp.int32).at[places].set(second_ints)  15.7 us
    scatter x1, local copies, waits for them, and re-layouts, fill_slots(): jnp.zeros((total_slots,), jnp.int32).at[places].set(first_ints)  15.7 us
    scatter x1, other arithmetic, fill_slots(): jnp.zeros((total_slots, payload.shape[1]), payload.dtype).at[places]  14.6 us
  transfers between devices with their start and end apart: 2, of which 1 were waited for; matrix products, arithmetic and copies ran while one was open for 7% of the time, Pallas kernels for 0%

commit v1 on v0

v1 whole, which is shorter than its diff:
```python
import jax
import jax.numpy as jnp
from jax import lax
from jax.experimental import pallas as pl
from jax.experimental.pallas import tpu as pltpu
from jax.sharding import Mesh
from jax.sharding import PartitionSpec as P

BLOCK = 128
TOPK = 16
SLOTS = 64
AREA = 72
DESTS = 128
BF = jnp.bfloat16
F32 = jnp.float32
I32 = jnp.int32
NT = (((1,), (1,)), ((), ()))
VMEM = pl.BlockSpec(memory_space=pltpu.VMEM)
SMEM = pl.BlockSpec(memory_space=pltpu.SMEM)


def pack_kernel(
    me_ref, bounds_ref, lengths_ref, measures_ref, preds_ref, dest_ref, keys_ref, groups_ref,
    own_ref, other_ref, area_ref, place_ref, place_smem, sem,
):
    rows = measures_ref.shape[0]
    wide = 2 * BLOCK
    half = DESTS // 2
    me = me_ref[0]
    lane = lax.broadcasted_iota(I32, (1, BLOCK), 1)
    before = (
        lax.broadcasted_iota(I32, (wide, wide), 0) < lax.broadcasted_iota(I32, (wide, wide), 1)
    ).astype(F32).astype(BF)
    count_of = jnp.concatenate([before, jnp.ones((wide, wide), BF)], axis=1)
    dest_ids = lax.broadcasted_iota(I32, (DESTS, wide), 0)
    slot_ids = lax.broadcasted_iota(I32, (SLOTS, wide), 0)
    carry = jnp.zeros((DESTS, wide), F32)
    packed = jnp.zeros((DESTS, 4 * SLOTS), F32)
    for step in range(rows // wide):
        parts = []
        for b in (2 * step, 2 * step + 1):
            at = pl.ds(b * BLOCK, BLOCK)
            ok = lane < lengths_ref[b]
            for c in range(preds_ref.shape[0]):
                v = preds_ref[c : c + 1, at]
                ok = ok & (v >= bounds_ref[c, 0]) & (v < bounds_ref[c, 1])
            d = dest_ref[b : b + 1, :]
            spot = ((d & 1) ^ me) * half + (d >> 1)
            parts.append(jnp.where(ok, spot, -1))
        target = jnp.concatenate(parts, axis=1)
        keys = jnp.concatenate([keys_ref[2 * step : 2 * step + 1, :], keys_ref[2 * step + 1 : 2 * step + 2, :]], axis=1)
        groups = jnp.concatenate([groups_ref[2 * step : 2 * step + 1, :], groups_ref[2 * step + 1 : 2 * step + 2, :]], axis=1)
        hit = dest_ids == target
        names = hit.astype(F32)
        names16 = names.astype(BF)
        counts = jnp.dot(names16, count_of, preferred_element_type=F32)
        slot = jnp.sum(names * (counts[:, :wide] + carry), axis=0, keepdims=True).astype(I32)
        carry = carry + counts[:, wide:]
        place = jnp.where(target >= 0, target * AREA + slot, DESTS * AREA)
        place_ref[2 * step : 2 * step + 1, :] = place[:, :BLOCK]
        place_ref[2 * step + 1 : 2 * step + 2, :] = place[:, BLOCK:]
        mine = slot_ids == slot
        values = [
            jnp.where(mine, part.astype(F32), 0.0).astype(BF)
            for part in (keys >> 8, keys & 255, groups >> 8, groups & 255)
        ]
        packed = packed + lax.dot_general(
            names16, jnp.concatenate(values, axis=0), NT, preferred_element_type=F32
        )
    copy = pltpu.make_async_copy(place_ref, place_smem, sem)
    copy.start()

    def clear(i, _):
        area_ref[pl.ds(pl.multiple_of(i * AREA, 8), AREA), :] = jnp.zeros((AREA, BLOCK), F32)
        return 0

    lax.fori_loop(0, DESTS, clear, 0, unroll=4)
    for d in range(DESTS):
        area_ref[d * AREA + SLOTS : d * AREA + SLOTS + 1, :] = packed[d : d + 1, :BLOCK]
        area_ref[d * AREA + SLOTS + 1 : d * AREA + SLOTS + 2, :] = packed[d : d + 1, BLOCK:]
    copy.wait()

    def put(i, _):
        x = measures_ref[pl.ds(pl.multiple_of(i * 16, 16), 16), :].astype(F32)
        for u in range(16):
            p = place_smem[i // 8, (i % 8) * 16 + u]
            area_ref[pl.ds(p, 1), :] = x[u : u + 1, :]
        return 0

    lax.fori_loop(0, rows // 16, put, 0, unroll=2)

    def give(i, _):
        at = pl.ds(pl.multiple_of(i * AREA, 8), AREA)
        own_ref[i] = area_ref[at, :].astype(BF)
        later = pl.ds(pl.multiple_of((i + half) * AREA, 8), AREA)
        other_ref[i] = area_ref[later, :].astype(BF)
        return 0

    lax.fori_loop(0, half, give, 0, unroll=2)


def pack(me, bounds, lengths, measures, preds, dest, keys, groups):
    half = DESTS // 2
    out = jax.ShapeDtypeStruct((half, AREA, BLOCK), BF)
    rows = measures.shape[0]
    return pl.pallas_call(
        pack_kernel,
        out_shape=(out, out),
        in_specs=[SMEM, SMEM, SMEM, VMEM, VMEM, VMEM, VMEM, VMEM],
        out_specs=(VMEM, VMEM),
        scratch_shapes=[
            pltpu.VMEM((DESTS * AREA + 8, BLOCK), F32),
            pltpu.VMEM((rows // BLOCK, BLOCK), I32),
            pltpu.SMEM((rows // BLOCK, BLOCK), I32),
            pltpu.SemaphoreType.DMA,
        ],
        compiler_params=pltpu.CompilerParams(vmem_limit_bytes=32 << 20),
        name="pack",
    )(me, bounds, lengths, measures, preds, dest, keys, groups)


def join_kernel(me_ref, got_ref, table_ref, own_ref, other_ref, pair_ref, sums_ref, keyt_ref, group_ref):
    chips = got_ref.shape[0]
    first = got_ref[:, SLOTS : SLOTS + 8, :].astype(F32)
    second = got_ref[:, AREA + SLOTS : AREA + SLOTS + 8, :].astype(F32)
    ka, kb = first[:, 0, :], second[:, 0, :]
    ga, gb = first[:, 1, :], second[:, 1, :]

    def halves(a, b):
        return (
            jnp.concatenate([a[:, :SLOTS], b[:, :SLOTS]], axis=1),
            jnp.concatenate([a[:, SLOTS:], b[:, SLOTS:]], axis=1),
        )

    key_hi, key_lo = halves(ka, kb)
    grp_hi, grp_lo = halves(ga, gb)
    square = jnp.zeros((BLOCK - chips, BLOCK), F32)
    keyt_ref[...] = jnp.concatenate([key_hi * 256.0 + key_lo, grp_hi], axis=0).T
    group_ref[0] = grp_hi
    group_ref[1] = grp_lo
    tab = jnp.concatenate([table_ref[:1024, :], table_ref[1024:, :]], axis=1)
    ids = lax.broadcasted_iota(I32, (BLOCK, 256), 1).astype(F32).astype(BF)
    one = jnp.ones((), BF)
    zero = jnp.zeros((), BF)
    for p in range(chips):
        key = jnp.broadcast_to(keyt_ref[:, p : p + 1], (BLOCK, BLOCK))
        top = jnp.broadcast_to(keyt_ref[:, chips + p : chips + p + 1], (BLOCK, BLOCK))
        upper = key >= 1024.0
        key = jnp.where(upper, key - 1024.0, key)
        cols = []
        for t in range(4):
            k = (key - 256.0 * t).astype(BF)
            k = jnp.concatenate([k, k], axis=1)
            cols.append(jnp.where(ids == k, one, zero))
        found = jnp.dot(jnp.concatenate(cols, axis=1), tab, preferred_element_type=F32)
        row = jnp.where(upper, found[:, BLOCK:], found[:, :BLOCK])
        pay = jnp.concatenate([got_ref[p, :SLOTS, :], got_ref[p, AREA : AREA + SLOTS, :]], axis=0)
        joined = pay.astype(F32) * row
        high = top >= 8.0
        none = jnp.zeros_like(joined)
        pair_ref[p * BLOCK : (p + 1) * BLOCK, :BLOCK] = jnp.where(high, none, joined).astype(BF)
        pair_ref[p * BLOCK : (p + 1) * BLOCK, BLOCK:] = jnp.where(high, joined, none).astype(BF)

    rows_at = lax.broadcasted_iota(I32, (256, BLOCK), 0).astype(F32).astype(BF)
    per = 8
    for k in range(chips // per):
        low3 = []
        for p in range(k * per, (k + 1) * per):
            hi = group_ref[0, p : p + 1, :]
            low3.append((jnp.where(hi >= 8.0, hi - 8.0, hi), group_ref[1, p : p + 1, :]))
        block = pair_ref[k * per * BLOCK : (k + 1) * per * BLOCK, :]
        for t in range(8):
            cols = []
            for hi, lo in low3:
                v = jnp.where(hi == float(t), lo, -1.0).astype(BF)
                cols.append(jnp.where(rows_at == jnp.broadcast_to(v, (256, BLOCK)), one, zero))
            part = jnp.dot(jnp.concatenate(cols, axis=1), block, preferred_element_type=F32)
            at = pl.ds(t * 256, 256)
            if k == 0:
                sums_ref[at, :] = part
            else:
                sums_ref[at, :] = sums_ref[at, :] + part

    me = me_ref[0]
    for i in range(64):
        col = (i // 32) * BLOCK
        base = (i % 32) * 64
        mine = pl.ds(pl.multiple_of(base + me * 32, 8), 32)
        theirs = pl.ds(pl.multiple_of(base + (1 - me) * 32, 8), 32)
        own_ref[i] = sums_ref[mine, col : col + BLOCK]
        other_ref[i] = sums_ref[theirs, col : col + BLOCK].astype(BF)


def join(me, got, table):
    chips = got.shape[0]
    return pl.pallas_call(
        join_kernel,
        out_shape=(
            jax.ShapeDtypeStruct((chips, 32, BLOCK), F32),
            jax.ShapeDtypeStruct((chips, 32, BLOCK), BF),
        ),
        in_specs=[SMEM, VMEM, VMEM],
        out_specs=(VMEM, VMEM),
        scratch_shapes=[
            pltpu.VMEM((chips * BLOCK, 2 * BLOCK), BF),
            pltpu.VMEM((2048, 2 * BLOCK), F32),
            pltpu.VMEM((BLOCK, BLOCK), F32),
            pltpu.VMEM((2, chips, BLOCK), F32),
        ],
        compiler_params=pltpu.CompilerParams(vmem_limit_bytes=40 << 20),
        name="join",
    )(me, got, table)


def merge_kernel(own_ref, got_ref, out_ref):
    chips, rows, _ = own_ref.shape
    total = (own_ref[...] + got_ref[...].astype(F32)).astype(BF)
    out_ref[:, :rows, :] = total
    ones = jnp.ones((8, BLOCK), BF)
    flat = total.reshape(chips * rows, BLOCK)
    means = lax.dot_general(ones, flat, NT, preferred_element_type=F32)
    score = jnp.concatenate(
        [means[0:1, n * BLOCK : (n + 1) * BLOCK] for n in range(chips * rows // BLOCK)], axis=0
    )
    score = (score * (1.0 / BLOCK)).astype(BF)
    out_ref[:, rows:, :] = jnp.broadcast_to(score[None], (chips, *score.shape))


def merge(own, got):
    chips, rows, _ = own.shape
    return pl.pallas_call(
        merge_kernel,
        out_shape=jax.ShapeDtypeStruct((chips, rows + chips * rows // BLOCK, BLOCK), BF),
        in_specs=[VMEM, VMEM],
        out_specs=VMEM,
        compiler_params=pltpu.CompilerParams(vmem_limit_bytes=16 << 20),
        name="merge",
    )(own, got)


def total_kernel(got_ref, sums_ref, score_ref):
    rows = sums_ref.shape[0]
    total = got_ref[0].astype(F32)
    for p in range(1, got_ref.shape[0]):
        total = total + got_ref[p].astype(F32)
    sums_ref[...] = total[:rows, :]
    score_ref[...] = total[rows:, :]


def total(got, rows):
    return pl.pallas_call(
        total_kernel,
        out_shape=(
            jax.ShapeDtypeStruct((rows, BLOCK), F32),
            jax.ShapeDtypeStruct((got.shape[1] - rows, BLOCK), F32),
        ),
        in_specs=[VMEM],
        out_specs=(VMEM, VMEM),
        compiler_params=pltpu.CompilerParams(vmem_limit_bytes=8 << 20),
        name="total",
    )(got)


def leaders_kernel(a_ref, b_ref, out_ref):
    x = jnp.concatenate([a_ref[...], b_ref[...]], axis=0)
    lane = lax.broadcasted_iota(I32, (1, BLOCK), 1)
    taken = jnp.zeros((1, 1), F32)
    out = jnp.full((1, BLOCK), -jnp.inf, F32)
    place = lane.astype(F32)
    for _ in range(TOPK):
        best = jnp.max(jnp.max(x, axis=0, keepdims=True), axis=1, keepdims=True)
        same = x == best
        count = jnp.sum(
            jnp.sum(same.astype(F32), axis=0, keepdims=True), axis=1, keepdims=True
        )
        out = jnp.where((place >= taken) & (place < taken + count), best, out)
        taken = taken + count
        x = jnp.where(same, -jnp.inf, x)
    out_ref[...] = out[:, :TOPK]


def leaders(a, b):
    return pl.pallas_call(
        leaders_kernel,
        out_shape=jax.ShapeDtypeStruct((1, TOPK), F32),
        in_specs=[VMEM, VMEM],
        out_specs=VMEM,
        compiler_params=pltpu.CompilerParams(vmem_limit_bytes=4 << 20),
        name="leaders",
    )(a, b)


CHIPS = ("section", "dom_0", "dom_1")
CORE = "dom_2"
DEVICES = (*CHIPS, CORE)
SWAP = [(0, 1), (1, 0)]


def on_device(
    measures, pred_columns, bounds, lengths, destination, key_offset, group_ids, build_table
):
    blocks = measures.shape[0] // BLOCK
    me = lax.axis_index(CORE).astype(I32).reshape(1)

    def lanes(v):
        return v.reshape(blocks, BLOCK)

    own, other = pack(
        me, bounds, lengths, measures, pred_columns, lanes(destination), lanes(key_offset), lanes(group_ids)
    )
    partner = lax.ppermute(other, CORE, SWAP)
    packets = jnp.concatenate([own, partner], axis=1)
    got = lax.all_to_all(packets, CHIPS, split_axis=0, concat_axis=0, tiled=True)
    mine, theirs = join(me, got, build_table)
    pair = merge(mine, lax.ppermute(theirs, CORE, SWAP))
    arrived = lax.all_to_all(pair, CHIPS, split_axis=0, concat_axis=0, tiled=True)
    group_sums, scores = total(arrived, 32)
    top = leaders(scores, lax.ppermute(scores, CORE, SWAP))
    return group_sums, top.reshape(TOPK)


def solution(mesh):
    finer = Mesh(mesh.devices.reshape(mesh.shape["section"], 4, 4, 2), DEVICES)
    return jax.shard_map(
        on_device,
        mesh=finer,
        in_specs=(
            P(DEVICES, None),
            P(None, DEVICES),
            P(),
            P(DEVICES),
            P(DEVICES, None),
            P(DEVICES),
            P(DEVICES),
            P(DEVICES, None),
        ),
        out_specs=(P(DEVICES, None), P()),
        check_vma=False,
    )
```

time: 217 us -> 113 us (0.52)
  matrix products: 60.8 us -> 0 us
  Pallas kernels: 0 us -> 32.7 us
  local copies, waits for them, and re-layouts: 35.8 us -> 5.47 us
  other arithmetic: 25.8 us -> 0.18 us
  waiting for transfers between devices: 29.6 us -> 4.84 us
  blocking collectives: 41.5 us -> 62.5 us
  starting transfers between devices: 21.7 us -> 5.85 us
    dot_general x16 -> x0, matrix products: 60.8 us -> none  [the longest x8 35.5 us: add_block(): jnp.dot(picker, joined_part, preferred_element_type=jnp.float32)]
    pallas_call x0 -> x5, Pallas kernels: none -> 32.7 us  [the longest x1 15 us: pack(): pl.pallas_call(pack_kernel, out_shape=(out, out), in_specs=[SMEM, SMEM, S...]
    scatter x2 -> x0, local copies, waits for them, and re-layouts: 31.4 us -> none  [the longest x1 15.7 us: fill_slots(): jnp.zeros((total_slots,), jnp.int32).at[places].set(second_ints)]
    all_to_all x2 -> x0, waiting for transfers between devices: 29.6 us -> none  [the longest x1 29.6 us: on_device(): lax.all_to_all(shaped[0], SECTION_DOM, split_axis=0, concat_axis=0, tiled...]
    all_to_all x2 -> x0, starting transfers between devices: 21.7 us -> none  [the longest x1 11.5 us: sent_together(): lax.all_to_all(both, axis, split_axis=split_dim, concat_axis=concat_dim,...]
    all_to_all x4 -> x2, blocking collectives: 41.5 us -> 62.5 us  [the longest x1 43 us: on_device(): lax.all_to_all(packets, CHIPS, split_axis=0, concat_axis=0, tiled=True)]
    scatter x1 -> x0, other arithmetic: 14.6 us -> none  [fill_slots(): jnp.zeros((total_slots, payload.shape[1]), payload.dtype).at[places]]
    top_k x1 -> x0, other arithmetic: 5.86 us -> none  [on_device(): leaders = lax.top_k(everything, TOPK)[0]]
  transfers between devices with their start and end apart: 2 -> 3, of which waited for: 1 -> 3; matrix products, arithmetic and copies ran while one was open for 7% -> 0% of each run, Pallas kernels for 0% -> 0%
where the time goes in v1:
time: 113 us; the launch traced here: 112 us
  blocking collectives  62.5 us (55%)
  Pallas kernels  32.7 us (29%)
  starting transfers between devices  5.85 us (5%)
  local copies, waits for them, and re-layouts  5.47 us (5%)
  waiting for transfers between devices  4.84 us (4%)
    all_to_all x1, blocking collectives, on_device(): lax.all_to_all(packets, CHIPS, split_axis=0, concat_axis=0, tiled=True)  43 us
    all_to_all x1, blocking collectives, on_device(): lax.all_to_all(pair, CHIPS, split_axis=0, concat_axis=0, tiled=True)  19.4 us
    pallas_call x1, Pallas kernels, pack(): pl.pallas_call(pack_kernel, out_shape=(out, out), in_specs=[SMEM, SMEM, S...  15 us
    pallas_call x1, Pallas kernels, join(): pl.pallas_call(join_kernel, out_shape=(jax.ShapeDtypeStruct((chips, 32, B...  14.7 us
    unnamed x16, local copies, waits for them, and re-layouts  5.47 us
    ppermute x1, waiting for transfers between devices, on_device(): partner = lax.ppermute(other, CORE, SWAP)  2.47 us
    ppermute x1, starting transfers between devices, on_device(): top = leaders(scores, lax.ppermute(scores, CORE, SWAP))  2.3 us
  transfers between devices with their start and end apart: 3, of which 3 were waited for; matrix products, arithmetic and copies ran while one was open for 0% of the time, Pallas kernels for 0%

profile of v1, /device:TPU:1, one launch (start us, length us, event | category | flops | bytes accessed | tf_op | source)
XLA Modules:
  0.0 112.2 jit_solution(2376449075656346459)
XLA Ops:
  0.6 0.0 copy-start
  0.6 1.2 %copy-done = bf16[4096,128]{1,0:T(8,128)(2,1)S(1)} copy-done((bf16[4096,128]{1,0:T(8,128)(2,1)S(1)}, bf16[4096,128]{1,0:T(8,128)(2,1)}, u32[]{:S(2)}) %copy-start) | copy-done | bytes 1048600
  1.9 0.0 copy-start.2
  1.9 0.8 copy-done.2
  2.6 0.0 copy-start.3
  2.6 0.7 copy-done.3
  3.3 0.0 copy-start.4
  3.3 0.7 copy-done.4
  4.1 0.0 copy-start.5
  4.1 0.7 copy-done.5
  4.8 0.0 copy-start.6
  4.8 0.7 copy-done.6
  5.5 0.0 copy-start.7
  5.5 0.7 copy-done.7
  6.1 15.0 %pack.1 = (bf16[64,72,128]{2,1,0:T(8,128)(2,1)S(1)}, bf16[64,72,128]{2,1,0:T(8,128)(2,1)S(1)}) custom-call(s32[1]{0:T(128)} %bitcast.me_ref, s32[2,2]{1,0:T(2,128)S(1)} %copy-done.6, s32[32]{0:T(128)S(1)} %copy-done.7, bf16[4096,128]{1,0:T(8,128)(2,1)S(1)} %copy-done, s32[2,4096]{1,0:T(2,128)S(1)} %copy-done.2, s32[32,128]{1,0:T(8,128)S(1)} %bitcast.5, ...), custom_call_target="tpu_custom_call" | custom-call | tf_op jit(solution)/shard_map/pack/pallas_call | solution.py:106
  21.1 1.5 %collective-permute-start = (bf16[64,72,128]{2,1,0:T(8,128)(2,1)S(1)}, bf16[64,72,128]{2,1,0:T(8,128)(2,1)S(1)}, u32[]{:S(2)}, u32[]{:S(2)}) collective-permute-start(bf16[64,72,128]{2,1,0:T(8,128)(2,1)S(1)} %get-tuple-element.9), channel_id=1, source_target_pairs={{0,1},{1,0},{2,3},{3,2},{4,5},{5,4},{6,7},{7,6},{8,9},{9,8},{10,11... | collective-permute-start | bytes 3538952 | tf_op jit(solution)/shard_map/ppermute | solution.py:311
  22.6 2.5 %collective-permute-done = bf16[64,72,128]{2,1,0:T(8,128)(2,1)S(1)} collective-permute-done((bf16[64,72,128]{2,1,0:T(8,128)(2,1)S(1)}, bf16[64,72,128]{2,1,0:T(8,128)(2,1)S(1)}, u32[]{:S(2)}, u32[]{:S(2)}) %collective-permute-start) | collective-permute-done | bytes 1179680 | tf_op jit(solution)/shard_map/ppermute | solution.py:311
  25.1 0.2 pad_maximum_fusion
  25.3 0.0 copy-start.1
  25.3 43.0 %all_to_all.10.got_ref = bf16[64,144,128]{2,1,0:T(8,128)(2,1)S(1)} all-to-all(bf16[64,144,128]{2,1,0:T(8,128)(2,1)S(1)} %pad_maximum_fusion), channel_id=1, replica_groups=mesh['section'=4,'dom_0'=4,'dom_1'=4,'dom_2'=2] {'section','dom_0','dom_1'}, dimensions={0} | all-to-all | bytes 4718592 | tf_op jit(solution)/shard_map/all_to_all | solution.py:313
  68.3 0.0 copy-done.1
  68.3 14.7 %join.1 = (f32[64,32,128]{2,1,0:T(8,128)S(1)}, bf16[64,32,128]{2,1,0:T(8,128)(2,1)S(1)}) custom-call(s32[1]{0:T(128)} %bitcast.me_ref, bf16[64,144,128]{2,1,0:T(8,128)(2,1)S(1)} %all_to_all.10.got_ref, bf16[2048,128]{1,0:T(8,128)(2,1)S(1)} %copy-done.1), custom_call_target="tpu_custom_call" | custom-call | tf_op jit(solution)/shard_map/join/pallas_call | solution.py:196
  83.0 2.1 %collective-permute-start.1 = (bf16[64,32,128]{2,1,0:T(8,128)(2,1)S(1)}, bf16[64,32,128]{2,1,0:T(8,128)(2,1)S(1)}, u32[]{:S(2)}, u32[]{:S(2)}) collective-permute-start(bf16[64,32,128]{2,1,0:T(8,128)(2,1)S(1)} %get-tuple-element.11), channel_id=1, source_target_pairs={{0,1},{1,0},{2,3},{3,2},{4,5},{5,4},{6,7},{7,6},{8,9},{9,8},{10,11... | collective-permute-start | bytes 1572872 | tf_op jit(solution)/shard_map/ppermute | solution.py:315
  85.1 1.5 %collective-permute-done.1.got_ref = bf16[64,32,128]{2,1,0:T(8,128)(2,1)S(1)} collective-permute-done((bf16[64,32,128]{2,1,0:T(8,128)(2,1)S(1)}, bf16[64,32,128]{2,1,0:T(8,128)(2,1)S(1)}, u32[]{:S(2)}, u32[]{:S(2)}) %collective-permute-start.1) | collective-permute-done | bytes 524320 | tf_op jit(solution)/shard_map/ppermute | solution.py:315
  86.7 0.3 merge.1
  87.0 19.4 %all_to_all.11.got_ref = bf16[64,48,128]{2,1,0:T(8,128)(2,1)S(1)} all-to-all(bf16[64,48,128]{2,1,0:T(8,128)(2,1)S(1)} %merge.1), channel_id=1, replica_groups=mesh['section'=4,'dom_0'=4,'dom_1'=4,'dom_2'=2] {'section','dom_0','dom_1'}, dimensions={0} | all-to-all | bytes 1572864 | tf_op jit(solution)/shard_map/all_to_all | solution.py:316
  106.4 0.7 total.1
  107.1 2.3 %collective-permute-start.2 = (f32[16,128]{1,0:T(8,128)S(1)}, f32[16,128]{1,0:T(8,128)S(1)}, u32[]{:S(2)}, u32[]{:S(2)}) collective-permute-start(f32[16,128]{1,0:T(8,128)S(1)} %get-tuple-element.13.a_ref), channel_id=1, source_target_pairs={{0,1},{1,0},{2,3},{3,2},{4,5},{5,4},{6,7},{7,6},{8,9},{9,8},{10,11... | collective-permute-start | bytes 24584 | tf_op jit(solution)/shard_map/ppermute | solution.py:318
  109.4 0.8 collective-permute-done.2.b_ref
  110.3 2.0 %leaders.1 = f32[1,16]{1,0:T(1,128)} custom-call(f32[16,128]{1,0:T(8,128)S(1)} %get-tuple-element.13.a_ref, f32[16,128]{1,0:T(8,128)S(1)} %collective-permute-done.2.b_ref), custom_call_target="tpu_custom_call" | custom-call | tf_op jit(solution)/shard_map/leaders/pallas_call | solution.py:283
Async XLA Ops:
  0.6 1.2 %copy-start = (bf16[4096,128]{1,0:T(8,128)(2,1)S(1)}, bf16[4096,128]{1,0:T(8,128)(2,1)}, u32[]{:S(2)}) copy-start(bf16[4096,128]{1,0:T(8,128)(2,1)} %measures_ref.1) | copy-start | bytes 3145732
  1.9 0.8 copy-start.2
  2.6 0.7 copy-start.3
  3.3 0.7 copy-start.4
  4.1 0.7 copy-start.5
  4.8 0.7 copy-start.6
  5.5 0.7 copy-start.7
  21.1 3.9 %collective-permute-start = (bf16[64,72,128]{2,1,0:T(8,128)(2,1)S(1)}, bf16[64,72,128]{2,1,0:T(8,128)(2,1)S(1)}, u32[]{:S(2)}, u32[]{:S(2)}) collective-permute-start(bf16[64,72,128]{2,1,0:T(8,128)(2,1)S(1)} %get-tuple-element.9), channel_id=1, source_target_pairs={{0,1},{1,0},{2,3},{3,2},{4,5},{5,4},{6,7},{7,6},{8,9},{9,8},{10,11... | collective-permute-start | bytes 3538952 | tf_op jit(solution)/shard_map/ppermute | solution.py:311
  25.3 43.0 %copy-start.1 = (bf16[2048,128]{1,0:T(8,128)(2,1)S(1)}, bf16[2048,128]{1,0:T(8,128)(2,1)}, u32[]{:S(2)}) copy-start(bf16[2048,128]{1,0:T(8,128)(2,1)} %table_ref.1) | copy-start | bytes 1572868
  83.0 3.6 %collective-permute-start.1 = (bf16[64,32,128]{2,1,0:T(8,128)(2,1)S(1)}, bf16[64,32,128]{2,1,0:T(8,128)(2,1)S(1)}, u32[]{:S(2)}, u32[]{:S(2)}) collective-permute-start(bf16[64,32,128]{2,1,0:T(8,128)(2,1)S(1)} %get-tuple-element.11), channel_id=1, source_target_pairs={{0,1},{1,0},{2,3},{3,2},{4,5},{5,4},{6,7},{7,6},{8,9},{9,8},{10,11... | collective-permute-start | bytes 1572872 | tf_op jit(solution)/shard_map/ppermute | solution.py:315
  107.1 3.1 %collective-permute-start.2 = (f32[16,128]{1,0:T(8,128)S(1)}, f32[16,128]{1,0:T(8,128)S(1)}, u32[]{:S(2)}, u32[]{:S(2)}) collective-permute-start(f32[16,128]{1,0:T(8,128)S(1)} %get-tuple-element.13.a_ref), channel_id=1, source_target_pairs={{0,1},{1,0},{2,3},{3,2},{4,5},{5,4},{6,7},{7,6},{8,9},{9,8},{10,11... | collective-permute-start | bytes 24584 | tf_op jit(solution)/shard_map/ppermute | solution.py:318

commit v2 on v1

--- a/solution.py
+++ b/solution.py
@@ -11,22 +11,39 @@
 SLOTS = 64
 AREA = 72
 DESTS = 128
+PIECES = 4
 BF = jnp.bfloat16
 F32 = jnp.float32
 I32 = jnp.int32
 NT = (((1,), (1,)), ((), ()))
 VMEM = pl.BlockSpec(memory_space=pltpu.VMEM)
 SMEM = pl.BlockSpec(memory_space=pltpu.SMEM)
+HBM = pl.BlockSpec(memory_space=pltpu.HBM)
 
 
 def pack_kernel(
-    me_ref, bounds_ref, lengths_ref, measures_ref, preds_ref, dest_ref, keys_ref, groups_ref,
-    own_ref, other_ref, area_ref, place_ref, place_smem, sem,
+    bounds_hbm, lengths_hbm, measures_hbm, preds_hbm, dest_hbm, keys_hbm, groups_hbm, out_hbm,
+    bounds_ref, lengths_ref, measures_ref, preds_ref, dest_ref, keys_ref, groups_ref,
+    area_ref, area16_ref, place_ref, place_smem, sems,
 ):
     rows = measures_ref.shape[0]
     wide = 2 * BLOCK
-    half = DESTS // 2
-    me = me_ref[0]
+    sources = (preds_hbm, dest_hbm, keys_hbm, groups_hbm, bounds_hbm, lengths_hbm, measures_hbm)
+    targets = (preds_ref, dest_ref, keys_ref, groups_ref, bounds_ref, lengths_ref, measures_ref)
+    loads = [
+        pltpu.make_async_copy(source, target, sems.at[n])
+        for n, (source, target) in enumerate(zip(sources, targets))
+    ]
+    for load in loads:
+        load.start()
+
+    def clear(i, _):
+        area_ref[pl.ds(pl.multiple_of(i * AREA, 8), AREA), :] = jnp.zeros((AREA, BLOCK), F32)
+        return 0
+
+    lax.fori_loop(0, DESTS, clear, 0, unroll=4)
+    for load in loads[:-1]:
+        load.wait()
     lane = lax.broadcasted_iota(I32, (1, BLOCK), 1)
     before = (
         lax.broadcasted_iota(I32, (wide, wide), 0) < lax.broadcasted_iota(I32, (wide, wide), 1)
@@ -36,27 +53,27 @@
     slot_ids = lax.broadcasted_iota(I32, (SLOTS, wide), 0)
     carry = jnp.zeros((DESTS, wide), F32)
     packed = jnp.zeros((DESTS, 4 * SLOTS), F32)
+
+    def pair(ref, step):
+        return jnp.concatenate(
+            [ref[2 * step : 2 * step + 1, :], ref[2 * step + 1 : 2 * step + 2, :]], axis=1
+        )
+
     for step in range(rows // wide):
-        parts = []
-        for b in (2 * step, 2 * step + 1):
-            at = pl.ds(b * BLOCK, BLOCK)
-            ok = lane < lengths_ref[b]
-            for c in range(preds_ref.shape[0]):
-                v = preds_ref[c : c + 1, at]
-                ok = ok & (v >= bounds_ref[c, 0]) & (v < bounds_ref[c, 1])
-            d = dest_ref[b : b + 1, :]
-            spot = ((d & 1) ^ me) * half + (d >> 1)
-            parts.append(jnp.where(ok, spot, -1))
-        target = jnp.concatenate(parts, axis=1)
-        keys = jnp.concatenate([keys_ref[2 * step : 2 * step + 1, :], keys_ref[2 * step + 1 : 2 * step + 2, :]], axis=1)
-        groups = jnp.concatenate([groups_ref[2 * step : 2 * step + 1, :], groups_ref[2 * step + 1 : 2 * step + 2, :]], axis=1)
-        hit = dest_ids == target
-        names = hit.astype(F32)
+        at = pl.ds(step * wide, wide)
+        ok = jnp.concatenate([lane < lengths_ref[2 * step], lane < lengths_ref[2 * step + 1]], axis=1)
+        for c in range(preds_ref.shape[0]):
+            v = preds_ref[c : c + 1, at]
+            ok = ok & (v >= bounds_ref[c, 0]) & (v < bounds_ref[c, 1])
+        target = jnp.where(ok, pair(dest_ref, step), -1)
+        keys = pair(keys_ref, step)
+        groups = pair(groups_ref, step)
+        names = (dest_ids == target).astype(F32)
         names16 = names.astype(BF)
         counts = jnp.dot(names16, count_of, preferred_element_type=F32)
         slot = jnp.sum(names * (counts[:, :wide] + carry), axis=0, keepdims=True).astype(I32)
         carry = carry + counts[:, wide:]
-        place = jnp.where(target >= 0, target * AREA + slot, DESTS * AREA)
+        place = jnp.where(ok, target * AREA + slot, DESTS * AREA)
         place_ref[2 * step : 2 * step + 1, :] = place[:, :BLOCK]
         place_ref[2 * step + 1 : 2 * step + 2, :] = place[:, BLOCK:]
         mine = slot_ids == slot
@@ -67,62 +84,72 @@
         packed = packed + lax.dot_general(
             names16, jnp.concatenate(values, axis=0), NT, preferred_element_type=F32
         )
-    copy = pltpu.make_async_copy(place_ref, place_smem, sem)
+    copy = pltpu.make_async_copy(place_ref, place_smem, sems.at[len(loads)])
     copy.start()
-
-    def clear(i, _):
-        area_ref[pl.ds(pl.multiple_of(i * AREA, 8), AREA), :] = jnp.zeros((AREA, BLOCK), F32)
-        return 0
-
-    lax.fori_loop(0, DESTS, clear, 0, unroll=4)
     for d in range(DESTS):
         area_ref[d * AREA + SLOTS : d * AREA + SLOTS + 1, :] = packed[d : d + 1, :BLOCK]
         area_ref[d * AREA + SLOTS + 1 : d * AREA + SLOTS + 2, :] = packed[d : d + 1, BLOCK:]
+    loads[-1].wait()
     copy.wait()
 
-    def put(i, _):
-        x = measures_ref[pl.ds(pl.multiple_of(i * 16, 16), 16), :].astype(F32)
-        for u in range(16):
-            p = place_smem[i // 8, (i % 8) * 16 + u]
-            area_ref[pl.ds(p, 1), :] = x[u : u + 1, :]
+    def put(b, _):
+        for k in range(BLOCK // 16):
+            x = measures_ref[pl.ds(pl.multiple_of(b * BLOCK + k * 16, 16), 16), :].astype(F32)
+            for u in range(16):
+                area_ref[pl.ds(place_smem[b, k * 16 + u], 1), :] = x[u : u + 1, :]
         return 0
 
-    lax.fori_loop(0, rows // 16, put, 0, unroll=2)
+    lax.fori_loop(0, rows // BLOCK, put, 0)
 
     def give(i, _):
-        at = pl.ds(pl.multiple_of(i * AREA, 8), AREA)
-        own_ref[i] = area_ref[at, :].astype(BF)
-        later = pl.ds(pl.multiple_of((i + half) * AREA, 8), AREA)
-        other_ref[i] = area_ref[later, :].astype(BF)
+        area16_ref[i] = area_ref[pl.ds(pl.multiple_of(i * AREA, 8), AREA), :].astype(BF)
         return 0
 
-    lax.fori_loop(0, half, give, 0, unroll=2)
-
-
-def pack(me, bounds, lengths, measures, preds, dest, keys, groups):
-    half = DESTS // 2
-    out = jax.ShapeDtypeStruct((half, AREA, BLOCK), BF)
+    stores = []
+    for n in range(PIECES):
+        part = DESTS // PIECES
+        lax.fori_loop(n * part, (n + 1) * part, give, 0, unroll=4)
+        stores.append(
+            pltpu.make_async_copy(
+                area16_ref.at[pl.ds(n * part, part)], out_hbm.at[pl.ds(n * part, part)], sems.at[8 + n]
+            )
+        )
+        stores[-1].start()
+    for store in stores:
+        store.wait()
+
+
+def pack(bounds, lengths, measures, preds, dest, keys, groups):
     rows = measures.shape[0]
+    blocks = rows // BLOCK
     return pl.pallas_call(
         pack_kernel,
-        out_shape=(out, out),
-        in_specs=[SMEM, SMEM, SMEM, VMEM, VMEM, VMEM, VMEM, VMEM],
-        out_specs=(VMEM, VMEM),
+        out_shape=jax.ShapeDtypeStruct((DESTS, AREA, BLOCK), BF),
+        in_specs=[HBM] * 7,
+        out_specs=HBM,
         scratch_shapes=[
+            pltpu.SMEM(bounds.shape, I32),
+            pltpu.SMEM(lengths.shape, I32),
+            pltpu.VMEM(measures.shape, BF),
+            pltpu.VMEM(preds.shape, I32),
+            pltpu.VMEM((blocks, BLOCK), I32),
+            pltpu.VMEM((blocks, BLOCK), I32),
+            pltpu.VMEM((blocks, BLOCK), I32),
             pltpu.VMEM((DESTS * AREA + 8, BLOCK), F32),
-            pltpu.VMEM((rows // BLOCK, BLOCK), I32),
-            pltpu.SMEM((rows // BLOCK, BLOCK), I32),
-            pltpu.SemaphoreType.DMA,
+            pltpu.VMEM((DESTS, AREA, BLOCK), BF),
+            pltpu.VMEM((blocks, BLOCK), I32),
+            pltpu.SMEM((blocks, BLOCK), I32),
+            pltpu.SemaphoreType.DMA((8 + PIECES,)),
         ],
-        compiler_params=pltpu.CompilerParams(vmem_limit_bytes=32 << 20),
+        compiler_params=pltpu.CompilerParams(vmem_limit_bytes=58 << 20),
         name="pack",
-    )(me, bounds, lengths, measures, preds, dest, keys, groups)
+    )(bounds, lengths, measures, preds, dest, keys, groups)
 
 
 def join_kernel(me_ref, got_ref, table_ref, own_ref, other_ref, pair_ref, sums_ref, keyt_ref, group_ref):
-    chips = got_ref.shape[0]
-    first = got_ref[:, SLOTS : SLOTS + 8, :].astype(F32)
-    second = got_ref[:, AREA + SLOTS : AREA + SLOTS + 8, :].astype(F32)
+    chips = got_ref.shape[0] // 2
+    first = got_ref[:chips, SLOTS : SLOTS + 8, :].astype(F32)
+    second = got_ref[chips:, SLOTS : SLOTS + 8, :].astype(F32)
     ka, kb = first[:, 0, :], second[:, 0, :]
     ga, gb = first[:, 1, :], second[:, 1, :]
 
@@ -134,7 +161,6 @@
 
     key_hi, key_lo = halves(ka, kb)
     grp_hi, grp_lo = halves(ga, gb)
-    square = jnp.zeros((BLOCK - chips, BLOCK), F32)
     keyt_ref[...] = jnp.concatenate([key_hi * 256.0 + key_lo, grp_hi], axis=0).T
     group_ref[0] = grp_hi
     group_ref[1] = grp_lo
@@ -154,7 +180,7 @@
             cols.append(jnp.where(ids == k, one, zero))
         found = jnp.dot(jnp.concatenate(cols, axis=1), tab, preferred_element_type=F32)
         row = jnp.where(upper, found[:, BLOCK:], found[:, :BLOCK])
-        pay = jnp.concatenate([got_ref[p, :SLOTS, :], got_ref[p, AREA : AREA + SLOTS, :]], axis=0)
+        pay = jnp.concatenate([got_ref[p, :SLOTS, :], got_ref[chips + p, :SLOTS, :]], axis=0)
         joined = pay.astype(F32) * row
         high = top >= 8.0
         none = jnp.zeros_like(joined)
@@ -192,7 +218,7 @@
 
 
 def join(me, got, table):
-    chips = got.shape[0]
+    chips = got.shape[0] // 2
     return pl.pallas_call(
         join_kernel,
         out_shape=(
@@ -305,12 +331,11 @@
     def lanes(v):
         return v.reshape(blocks, BLOCK)
 
-    own, other = pack(
-        me, bounds, lengths, measures, pred_columns, lanes(destination), lanes(key_offset), lanes(group_ids)
+    me, bounds = lax.optimization_barrier((me, bounds))
+    packets = pack(
+        bounds, lengths, measures, pred_columns, lanes(destination), lanes(key_offset), lanes(group_ids)
     )
-    partner = lax.ppermute(other, CORE, SWAP)
-    packets = jnp.concatenate([own, partner], axis=1)
-    got = lax.all_to_all(packets, CHIPS, split_axis=0, concat_axis=0, tiled=True)
+    got = lax.all_to_all(packets, DEVICES, split_axis=0, concat_axis=0, tiled=True)
     mine, theirs = join(me, got, build_table)
     pair = merge(mine, lax.ppermute(theirs, CORE, SWAP))
     arrived = lax.all_to_all(pair, CHIPS, split_axis=0, concat_axis=0, tiled=True)

time: 113 us -> 95.9 us (0.85)
  Pallas kernels: 32.7 us -> 25.7 us
  local copies, waits for them, and re-layouts: 5.47 us -> 0.01 us
  waiting for transfers between devices: 4.84 us -> 2.37 us
  starting transfers between devices: 5.85 us -> 3.62 us
    pallas_call x1, Pallas kernels: 15 us -> 8.34 us  [pack(): pl.pallas_call(pack_kernel, out_shape=jax.ShapeDtypeStruct((DESTS, AREA,...]
    unnamed x16 -> x2, local copies, waits for them, and re-layouts: 5.47 us -> 0.01 us
    ppermute x1 -> x0, waiting for transfers between devices: 2.47 us -> none  [on_device(): partner = lax.ppermute(other, CORE, SWAP)]
    all_to_all x1, blocking collectives: 43 us -> 44.5 us  [on_device(): lax.all_to_all(packets, DEVICES, split_axis=0, concat_axis=0, tiled=True)]
    ppermute x1 -> x0, starting transfers between devices: 1.46 us -> none  [on_device(): partner = lax.ppermute(other, CORE, SWAP)]
  transfers between devices with their start and end apart: 3 -> 2, of which waited for: 3 -> 2; matrix products, arithmetic and copies ran while one was open for 0% -> 0% of each run, Pallas kernels for 0% -> 0%
where the time goes in v2:
time: 95.9 us; the launch traced here: 95.7 us
  blocking collectives  63.3 us (66%)
  Pallas kernels  25.7 us (27%)
  starting transfers between devices  3.62 us (4%)
  waiting for transfers between devices  2.37 us (2%)
    all_to_all x1, blocking collectives, on_device(): lax.all_to_all(packets, DEVICES, split_axis=0, concat_axis=0, tiled=True)  44.5 us
    all_to_all x1, blocking collectives, on_device(): lax.all_to_all(pair, CHIPS, split_axis=0, concat_axis=0, tiled=True)  18.7 us
    pallas_call x1, Pallas kernels, join(): pl.pallas_call(join_kernel, out_shape=(jax.ShapeDtypeStruct((chips, 32, B...  14.4 us
    pallas_call x1, Pallas kernels, pack(): pl.pallas_call(pack_kernel, out_shape=jax.ShapeDtypeStruct((DESTS, AREA,...  8.34 us
    ppermute x1, starting transfers between devices, on_device(): top = leaders(scores, lax.ppermute(scores, CORE, SWAP))  2.3 us
    pallas_call x1, Pallas kernels, leaders(): pl.pallas_call(leaders_kernel, out_shape=jax.ShapeDtypeStruct((1, TOPK),...  1.95 us
  transfers between devices with their start and end apart: 2, of which 2 were waited for; matrix products, arithmetic and copies ran while one was open for 0% of the time, Pallas kernels for 0%

profile of v2, /device:TPU:1, one launch (start us, length us, event | category | flops | bytes accessed | tf_op | source)
XLA Modules:
  0.0 95.7 jit_solution(7036695178494686939)
XLA Ops:
  0.6 8.3 %pack.1 = bf16[128,72,128]{2,1,0:T(8,128)(2,1)} custom-call(s32[2,2]{1,0:T(2,128)} %bounds_hbm, s32[32]{0:T(128)} %lengths_hbm.1, bf16[4096,128]{1,0:T(8,128)(2,1)} %measures_hbm.1, s32[2,4096]{1,0:T(2,128)} %preds_hbm.1, s32[32,128]{1,0:T(8,128)} %bitcast.5, s32[32,128]{1,0:T(8,128)} %bitcast.6, s32[32,128]{1,0:T(8,128)} %bitcast.7), custom_call_target="tpu_custom_call" | custom-call | tf_op jit(solution)/shard_map/pack/pallas_call | solution.py:125
  9.0 0.0 copy-start
  9.0 44.5 %all_to_all.10.got_ref = bf16[128,72,128]{2,1,0:T(8,128)(2,1)S(1)} all-to-all(bf16[128,72,128]{2,1,0:T(8,128)(2,1)} %pack.1), channel_id=1, replica_groups=mesh['section'=4,'dom_0'=4,'dom_1'=4,'dom_2'=2] {'section','dom_0','dom_..., dimensions={0} | all-to-all | bytes 4718592 | tf_op jit(solution)/shard_map/all_to_all | solution.py:338
  53.5 0.0 copy-done
  53.5 14.4 %join.1 = (f32[64,32,128]{2,1,0:T(8,128)S(1)}, bf16[64,32,128]{2,1,0:T(8,128)(2,1)S(1)}) custom-call(s32[1]{0:T(128)} %bitcast.me_ref, bf16[128,72,128]{2,1,0:T(8,128)(2,1)S(1)} %all_to_all.10.got_ref, bf16[2048,128]{1,0:T(8,128)(2,1)S(1)} %copy-done), custom_call_target="tpu_custom_call" | custom-call | tf_op jit(solution)/shard_map/join/pallas_call | solution.py:222
  68.0 1.3 %collective-permute-start = (bf16[64,32,128]{2,1,0:T(8,128)(2,1)S(1)}, bf16[64,32,128]{2,1,0:T(8,128)(2,1)S(1)}, u32[]{:S(2)}, u32[]{:S(2)}) collective-permute-start(bf16[64,32,128]{2,1,0:T(8,128)(2,1)S(1)} %get-tuple-element.11), channel_id=1, source_target_pairs={{0,1},{1,0},{2,3},{3,2},{4,5},{5,4},{6,7},{7,6},{8,9},{9,8},{10,11... | collective-permute-start | bytes 1572872 | tf_op jit(solution)/shard_map/ppermute | solution.py:340
  69.3 1.5 %collective-permute-done.got_ref = bf16[64,32,128]{2,1,0:T(8,128)(2,1)S(1)} collective-permute-done((bf16[64,32,128]{2,1,0:T(8,128)(2,1)S(1)}, bf16[64,32,128]{2,1,0:T(8,128)(2,1)S(1)}, u32[]{:S(2)}, u32[]{:S(2)}) %collective-permute-start) | collective-permute-done | bytes 524320 | tf_op jit(solution)/shard_map/ppermute | solution.py:340
  70.8 0.3 merge.1
  71.1 18.7 %all_to_all.11.got_ref = bf16[64,48,128]{2,1,0:T(8,128)(2,1)S(1)} all-to-all(bf16[64,48,128]{2,1,0:T(8,128)(2,1)S(1)} %merge.1), channel_id=1, replica_groups=mesh['section'=4,'dom_0'=4,'dom_1'=4,'dom_2'=2] {'section','dom_0','dom_1'}, dimensions={0} | all-to-all | bytes 1572864 | tf_op jit(solution)/shard_map/all_to_all | solution.py:341
  89.9 0.7 total.1
  90.6 2.3 %collective-permute-start.1 = (f32[16,128]{1,0:T(8,128)S(1)}, f32[16,128]{1,0:T(8,128)S(1)}, u32[]{:S(2)}, u32[]{:S(2)}) collective-permute-start(f32[16,128]{1,0:T(8,128)S(1)} %get-tuple-element.13.a_ref), channel_id=1, source_target_pairs={{0,1},{1,0},{2,3},{3,2},{4,5},{5,4},{6,7},{7,6},{8,9},{9,8},{10,11... | collective-permute-start | bytes 24584 | tf_op jit(solution)/shard_map/ppermute | solution.py:343
  92.9 0.8 collective-permute-done.1.b_ref
  93.7 2.0 %leaders.1 = f32[1,16]{1,0:T(1,128)} custom-call(f32[16,128]{1,0:T(8,128)S(1)} %get-tuple-element.13.a_ref, f32[16,128]{1,0:T(8,128)S(1)} %collective-permute-done.1.b_ref), custom_call_target="tpu_custom_call" | custom-call | tf_op jit(solution)/shard_map/leaders/pallas_call | solution.py:309
Async XLA Ops:
  9.0 44.6 %copy-start = (bf16[2048,128]{1,0:T(8,128)(2,1)S(1)}, bf16[2048,128]{1,0:T(8,128)(2,1)}, u32[]{:S(2)}) copy-start(bf16[2048,128]{1,0:T(8,128)(2,1)} %table_ref.1) | copy-start | bytes 1572868
  68.0 2.9 %collective-permute-start = (bf16[64,32,128]{2,1,0:T(8,128)(2,1)S(1)}, bf16[64,32,128]{2,1,0:T(8,128)(2,1)S(1)}, u32[]{:S(2)}, u32[]{:S(2)}) collective-permute-start(bf16[64,32,128]{2,1,0:T(8,128)(2,1)S(1)} %get-tuple-element.11), channel_id=1, source_target_pairs={{0,1},{1,0},{2,3},{3,2},{4,5},{5,4},{6,7},{7,6},{8,9},{9,8},{10,11... | collective-permute-start | bytes 1572872 | tf_op jit(solution)/shard_map/ppermute | solution.py:340
  90.6 3.1 %collective-permute-start.1 = (f32[16,128]{1,0:T(8,128)S(1)}, f32[16,128]{1,0:T(8,128)S(1)}, u32[]{:S(2)}, u32[]{:S(2)}) collective-permute-start(f32[16,128]{1,0:T(8,128)S(1)} %get-tuple-element.13.a_ref), channel_id=1, source_target_pairs={{0,1},{1,0},{2,3},{3,2},{4,5},{5,4},{6,7},{7,6},{8,9},{9,8},{10,11... | collective-permute-start | bytes 24584 | tf_op jit(solution)/shard_map/ppermute | solution.py:343

commit v3 on v2

--- a/solution.py
+++ b/solution.py
@@ -9,9 +9,12 @@
 BLOCK = 128
 TOPK = 16
 SLOTS = 64
-AREA = 72
 DESTS = 128
+AREA = 66
+FLAT = DESTS * AREA
+ROWS = DESTS * SLOTS
 PIECES = 4
+SPAN = 1024
 BF = jnp.bfloat16
 F32 = jnp.float32
 I32 = jnp.int32
@@ -38,10 +41,10 @@
         load.start()
 
     def clear(i, _):
-        area_ref[pl.ds(pl.multiple_of(i * AREA, 8), AREA), :] = jnp.zeros((AREA, BLOCK), F32)
-        return 0
-
-    lax.fori_loop(0, DESTS, clear, 0, unroll=4)
+        area_ref[pl.ds(pl.multiple_of(i * 64, 64), 64), :] = jnp.zeros((64, BLOCK), F32)
+        return 0
+
+    lax.fori_loop(0, FLAT // 64, clear, 0, unroll=4)
     for load in loads[:-1]:
         load.wait()
     lane = lax.broadcasted_iota(I32, (1, BLOCK), 1)
@@ -73,13 +76,13 @@
         counts = jnp.dot(names16, count_of, preferred_element_type=F32)
         slot = jnp.sum(names * (counts[:, :wide] + carry), axis=0, keepdims=True).astype(I32)
         carry = carry + counts[:, wide:]
-        place = jnp.where(ok, target * AREA + slot, DESTS * AREA)
+        place = jnp.where(ok, target * AREA + slot, FLAT)
         place_ref[2 * step : 2 * step + 1, :] = place[:, :BLOCK]
         place_ref[2 * step + 1 : 2 * step + 2, :] = place[:, BLOCK:]
         mine = slot_ids == slot
         values = [
             jnp.where(mine, part.astype(F32), 0.0).astype(BF)
-            for part in (keys >> 8, keys & 255, groups >> 8, groups & 255)
+            for part in ((keys >> 8) + 1, keys & 255, groups >> 8, groups & 255)
         ]
         packed = packed + lax.dot_general(
             names16, jnp.concatenate(values, axis=0), NT, preferred_element_type=F32
@@ -102,18 +105,16 @@
     lax.fori_loop(0, rows // BLOCK, put, 0)
 
     def give(i, _):
-        area16_ref[i] = area_ref[pl.ds(pl.multiple_of(i * AREA, 8), AREA), :].astype(BF)
+        at = pl.ds(pl.multiple_of(i * 64, 64), 64)
+        area16_ref[at, :] = area_ref[at, :].astype(BF)
         return 0
 
     stores = []
+    part = FLAT // PIECES
     for n in range(PIECES):
-        part = DESTS // PIECES
-        lax.fori_loop(n * part, (n + 1) * part, give, 0, unroll=4)
-        stores.append(
-            pltpu.make_async_copy(
-                area16_ref.at[pl.ds(n * part, part)], out_hbm.at[pl.ds(n * part, part)], sems.at[8 + n]
-            )
-        )
+        lax.fori_loop(n * part // 64, (n + 1) * part // 64, give, 0, unroll=3)
+        at = pl.ds(n * part, part)
+        stores.append(pltpu.make_async_copy(area16_ref.at[at], out_hbm.at[at], sems.at[8 + n]))
         stores[-1].start()
     for store in stores:
         store.wait()
@@ -124,7 +125,7 @@
     blocks = rows // BLOCK
     return pl.pallas_call(
         pack_kernel,
-        out_shape=jax.ShapeDtypeStruct((DESTS, AREA, BLOCK), BF),
+        out_shape=jax.ShapeDtypeStruct((FLAT, BLOCK), BF),
         in_specs=[HBM] * 7,
         out_specs=HBM,
         scratch_shapes=[
@@ -135,8 +136,8 @@
             pltpu.VMEM((blocks, BLOCK), I32),
             pltpu.VMEM((blocks, BLOCK), I32),
             pltpu.VMEM((blocks, BLOCK), I32),
-            pltpu.VMEM((DESTS * AREA + 8, BLOCK), F32),
-            pltpu.VMEM((DESTS, AREA, BLOCK), BF),
+            pltpu.VMEM((FLAT + 8, BLOCK), F32),
+            pltpu.VMEM((FLAT, BLOCK), BF),
             pltpu.VMEM((blocks, BLOCK), I32),
             pltpu.SMEM((blocks, BLOCK), I32),
             pltpu.SemaphoreType.DMA((8 + PIECES,)),
@@ -146,67 +147,91 @@
     )(bounds, lengths, measures, preds, dest, keys, groups)
 
 
-def join_kernel(me_ref, got_ref, table_ref, own_ref, other_ref, pair_ref, sums_ref, keyt_ref, group_ref):
-    chips = got_ref.shape[0] // 2
-    first = got_ref[:chips, SLOTS : SLOTS + 8, :].astype(F32)
-    second = got_ref[chips:, SLOTS : SLOTS + 8, :].astype(F32)
-    ka, kb = first[:, 0, :], second[:, 0, :]
-    ga, gb = first[:, 1, :], second[:, 1, :]
-
-    def halves(a, b):
-        return (
-            jnp.concatenate([a[:, :SLOTS], b[:, :SLOTS]], axis=1),
-            jnp.concatenate([a[:, SLOTS:], b[:, SLOTS:]], axis=1),
-        )
-
-    key_hi, key_lo = halves(ka, kb)
-    grp_hi, grp_lo = halves(ga, gb)
-    keyt_ref[...] = jnp.concatenate([key_hi * 256.0 + key_lo, grp_hi], axis=0).T
-    group_ref[0] = grp_hi
-    group_ref[1] = grp_lo
+def join_kernel(
+    me_ref, got_ref, table_ref, own_ref, other_ref,
+    pay_ref, side_ref, aux_ref, turned_ref, base_ref, base_smem, pair_ref, sums_ref, sem,
+):
+    for s in range(DESTS):
+        pair = got_ref[s * AREA + SLOTS : (s + 1) * AREA, :].astype(F32)
+        aux_ref[:, s : s + 1, :] = pair.reshape(2, 1, BLOCK)
+    key_hi = aux_ref[0, :, :SLOTS]
+    live = (key_hi > 0.0).astype(F32).astype(BF)
+    counts = lax.dot_general(jnp.ones((8, SLOTS), BF), live, NT, preferred_element_type=F32)
+    earlier = (
+        lax.broadcasted_iota(I32, (DESTS, DESTS), 0) < lax.broadcasted_iota(I32, (DESTS, DESTS), 1)
+    ).astype(F32).astype(BF)
+    starts = jnp.dot(counts.astype(BF), earlier, preferred_element_type=F32)
+    row = lax.broadcasted_iota(I32, (8, DESTS), 0)
+    base_ref[...] = jnp.where(row == 0, starts, starts + counts).astype(I32)
+    copy = pltpu.make_async_copy(base_ref, base_smem, sem)
+    copy.start()
+    key = (key_hi - 1.0) * 256.0 + aux_ref[0, :, SLOTS:]
+    group = aux_ref[1, :, :SLOTS] * 256.0 + aux_ref[1, :, SLOTS:]
+    code = key * 4096.0 + group
+    turned_ref[...] = jnp.concatenate([code, code], axis=1).T
+    sums_ref[...] = jnp.zeros_like(sums_ref)
+    copy.wait()
+    total = base_smem[1, DESTS - 1]
+    for s in range(DESTS):
+        at = pl.ds(base_smem[0, s], SLOTS)
+        pay_ref[at, :] = got_ref[s * AREA : s * AREA + SLOTS, :].astype(F32)
+        side_ref[at, :] = jnp.broadcast_to(turned_ref[:SLOTS, s : s + 1], (SLOTS, BLOCK))
     tab = jnp.concatenate([table_ref[:1024, :], table_ref[1024:, :]], axis=1)
     ids = lax.broadcasted_iota(I32, (BLOCK, 256), 1).astype(F32).astype(BF)
+    rows_at = lax.broadcasted_iota(I32, (256, BLOCK), 0).astype(F32).astype(BF)
+    spot = lax.broadcasted_iota(I32, (BLOCK, BLOCK), 0)
     one = jnp.ones((), BF)
     zero = jnp.zeros((), BF)
-    for p in range(chips):
-        key = jnp.broadcast_to(keyt_ref[:, p : p + 1], (BLOCK, BLOCK))
-        top = jnp.broadcast_to(keyt_ref[:, chips + p : chips + p + 1], (BLOCK, BLOCK))
-        upper = key >= 1024.0
-        key = jnp.where(upper, key - 1024.0, key)
-        cols = []
-        for t in range(4):
-            k = (key - 256.0 * t).astype(BF)
-            k = jnp.concatenate([k, k], axis=1)
-            cols.append(jnp.where(ids == k, one, zero))
-        found = jnp.dot(jnp.concatenate(cols, axis=1), tab, preferred_element_type=F32)
-        row = jnp.where(upper, found[:, BLOCK:], found[:, :BLOCK])
-        pay = jnp.concatenate([got_ref[p, :SLOTS, :], got_ref[chips + p, :SLOTS, :]], axis=0)
-        joined = pay.astype(F32) * row
-        high = top >= 8.0
-        none = jnp.zeros_like(joined)
-        pair_ref[p * BLOCK : (p + 1) * BLOCK, :BLOCK] = jnp.where(high, none, joined).astype(BF)
-        pair_ref[p * BLOCK : (p + 1) * BLOCK, BLOCK:] = jnp.where(high, joined, none).astype(BF)
-
-    rows_at = lax.broadcasted_iota(I32, (256, BLOCK), 0).astype(F32).astype(BF)
-    per = 8
-    for k in range(chips // per):
-        low3 = []
-        for p in range(k * per, (k + 1) * per):
-            hi = group_ref[0, p : p + 1, :]
-            low3.append((jnp.where(hi >= 8.0, hi - 8.0, hi), group_ref[1, p : p + 1, :]))
-        block = pair_ref[k * per * BLOCK : (k + 1) * per * BLOCK, :]
+
+    def block(start, span):
+        lows = []
+        for n in range(span // BLOCK):
+            first = pl.multiple_of(start + n * BLOCK, BLOCK)
+            side = side_ref[pl.ds(first, BLOCK), :]
+            key = jnp.floor(side * (1.0 / 4096.0))
+            high = side - key * 4096.0 >= 2048.0
+            group = side.T[:1, :]
+            group = group - jnp.floor(group * (1.0 / 4096.0)) * 4096.0
+            lows.append(jnp.where(group >= 2048.0, group - 2048.0, group))
+            upper = key >= 1024.0
+            key = jnp.where(upper, key - 1024.0, key)
+            cols = []
+            for t in range(4):
+                k = (key - 256.0 * t).astype(BF)
+                k = jnp.concatenate([k, k], axis=1)
+                cols.append(jnp.where(ids == k, one, zero))
+            found = jnp.dot(jnp.concatenate(cols, axis=1), tab, preferred_element_type=F32)
+            found = jnp.where(upper, found[:, BLOCK:], found[:, :BLOCK])
+            joined = pay_ref[pl.ds(first, BLOCK), :] * found
+            none = jnp.zeros_like(joined)
+            joined = jnp.where(first + spot < total, joined, none)
+            to = pl.ds(n * BLOCK, BLOCK)
+            pair_ref[to, :BLOCK] = jnp.where(high, none, joined).astype(BF)
+            pair_ref[to, BLOCK:] = jnp.where(high, joined, none).astype(BF)
         for t in range(8):
-            cols = []
-            for hi, lo in low3:
-                v = jnp.where(hi == float(t), lo, -1.0).astype(BF)
-                cols.append(jnp.where(rows_at == jnp.broadcast_to(v, (256, BLOCK)), one, zero))
-            part = jnp.dot(jnp.concatenate(cols, axis=1), block, preferred_element_type=F32)
+            cols = [
+                jnp.where(
+                    rows_at == jnp.broadcast_to((low - 256.0 * t).astype(BF), (256, BLOCK)), one, zero
+                )
+                for low in lows
+            ]
             at = pl.ds(t * 256, 256)
-            if k == 0:
-                sums_ref[at, :] = part
-            else:
-                sums_ref[at, :] = sums_ref[at, :] + part
-
+            sums_ref[at, :] += jnp.dot(
+                jnp.concatenate(cols, axis=1), pair_ref[:span, :], preferred_element_type=F32
+            )
+
+    wide = total // SPAN * SPAN
+
+    def wide_block(b, _):
+        block(b * SPAN, SPAN)
+        return 0
+
+    def narrow_block(b, _):
+        block(wide + b * (SPAN // 2), SPAN // 2)
+        return 0
+
+    lax.fori_loop(0, total // SPAN, wide_block, 0)
+    lax.fori_loop(0, (total - wide + SPAN // 2 - 1) // (SPAN // 2), narrow_block, 0)
     me = me_ref[0]
     for i in range(64):
         col = (i // 32) * BLOCK
@@ -218,20 +243,24 @@
 
 
 def join(me, got, table):
-    chips = got.shape[0] // 2
     return pl.pallas_call(
         join_kernel,
         out_shape=(
-            jax.ShapeDtypeStruct((chips, 32, BLOCK), F32),
-            jax.ShapeDtypeStruct((chips, 32, BLOCK), BF),
+            jax.ShapeDtypeStruct((64, 32, BLOCK), F32),
+            jax.ShapeDtypeStruct((64, 32, BLOCK), BF),
         ),
         in_specs=[SMEM, VMEM, VMEM],
         out_specs=(VMEM, VMEM),
         scratch_shapes=[
-            pltpu.VMEM((chips * BLOCK, 2 * BLOCK), BF),
+            pltpu.VMEM((ROWS, BLOCK), F32),
+            pltpu.VMEM((ROWS, BLOCK), F32),
+            pltpu.VMEM((2, DESTS, BLOCK), F32),
+            pltpu.VMEM((BLOCK, BLOCK), F32),
+            pltpu.VMEM((8, DESTS), I32),
+            pltpu.SMEM((8, DESTS), I32),
+            pltpu.VMEM((SPAN, 2 * BLOCK), BF),
             pltpu.VMEM((2048, 2 * BLOCK), F32),
-            pltpu.VMEM((BLOCK, BLOCK), F32),
-            pltpu.VMEM((2, chips, BLOCK), F32),
+            pltpu.SemaphoreType.DMA,
         ],
         compiler_params=pltpu.CompilerParams(vmem_limit_bytes=40 << 20),
         name="join",
@@ -335,7 +364,9 @@
     packets = pack(
         bounds, lengths, measures, pred_columns, lanes(destination), lanes(key_offset), lanes(group_ids)
     )
-    got = lax.all_to_all(packets, DEVICES, split_axis=0, concat_axis=0, tiled=True)
+    got = lax.all_to_all(
+        packets.reshape(DESTS, AREA // 2, 2, BLOCK), DEVICES, split_axis=0, concat_axis=0, tiled=True
+    ).reshape(FLAT, BLOCK)
     mine, theirs = join(me, got, build_table)
     pair = merge(mine, lax.ppermute(theirs, CORE, SWAP))
     arrived = lax.all_to_all(pair, CHIPS, split_axis=0, concat_axis=0, tiled=True)

time: 95.9 us -> 96 us (level)
  Pallas kernels: 25.7 us -> 28.4 us
  blocking collectives: 63.3 us -> 61.3 us
  starting transfers between devices: 3.62 us -> 2.38 us
    pallas_call x2, Pallas kernels: 22.8 us -> 25.5 us  [the longest x1 17.2 us: join(): pl.pallas_call(join_kernel, out_shape=(jax.ShapeDtypeStruct((64, 32, BLOC...]
    all_to_all x1, blocking collectives: 44.5 us -> 42.4 us  [on_device(): lax.all_to_all(packets.reshape(DESTS, AREA // 2, 2, BLOCK), DEVICES, spli...]
    ppermute x1, starting transfers between devices: 1.32 us -> 0.09 us  [on_device(): pair = merge(mine, lax.ppermute(theirs, CORE, SWAP))]
where the time goes in v3:
time: 96 us; the launch traced here: 95.5 us
  blocking collectives  61.3 us (64%)
  Pallas kernels  28.4 us (30%)
  waiting for transfers between devices  2.73 us (3%)
  starting transfers between devices  2.38 us (2%)
    all_to_all x1, blocking collectives, on_device(): lax.all_to_all(packets.reshape(DESTS, AREA // 2, 2, BLOCK), DEVICES, spli...  42.4 us
    all_to_all x1, blocking collectives, on_device(): lax.all_to_all(pair, CHIPS, split_axis=0, concat_axis=0, tiled=True)  18.9 us
    pallas_call x1, Pallas kernels, join(): pl.pallas_call(join_kernel, out_shape=(jax.ShapeDtypeStruct((64, 32, BLOC...  17.2 us
    pallas_call x1, Pallas kernels, pack(): pl.pallas_call(pack_kernel, out_shape=jax.ShapeDtypeStruct((FLAT, BLOCK),...  8.3 us
    ppermute x1, starting transfers between devices, on_device(): top = leaders(scores, lax.ppermute(scores, CORE, SWAP))  2.3 us
    pallas_call x1, Pallas kernels, leaders(): pl.pallas_call(leaders_kernel, out_shape=jax.ShapeDtypeStruct((1, TOPK),...  1.95 us
  transfers between devices with their start and end apart: 2, of which 2 were waited for; matrix products, arithmetic and copies ran while one was open for 0% of the time, Pallas kernels for 0%

profile of v3, /device:TPU:1, one launch (start us, length us, event | category | flops | bytes accessed | tf_op | source)
XLA Modules:
  0.0 95.5 jit_solution(12610024499307097007)
XLA Ops:
  0.6 8.3 %pack.1 = bf16[8448,128]{1,0:T(8,128)(2,1)} custom-call(s32[2,2]{1,0:T(2,128)} %bounds_hbm, s32[32]{0:T(128)} %lengths_hbm.1, bf16[4096,128]{1,0:T(8,128)(2,1)} %measures_hbm.1, s32[2,4096]{1,0:T(2,128)} %preds_hbm.1, s32[32,128]{1,0:T(8,128)} %bitcast.9, s32[32,128]{1,0:T(8,128)} %bitcast.10, s32[32,128]{1,0:T(8,128)} %bitcast.11), custom_call_target="tpu_custom_call" | custom-call | tf_op jit(solution)/shard_map/pack/pallas_call | solution.py:126
  8.9 0.0 copy-start
  9.0 42.4 %all_to_all.10 = bf16[128,33,2,128]{3,2,1,0:T(2,128)(2,1)S(1)} all-to-all(bf16[128,33,2,128]{3,2,1,0:T(2,128)(2,1)} %bitcast.8), channel_id=1, replica_groups=mesh['section'=4,'dom_0'=4,'dom_1'=4,'dom_2'=2] {'section','dom_0','dom_..., dimensions={0} | all-to-all | bytes 4325376 | tf_op jit(solution)/shard_map/all_to_all | solution.py:367
  51.4 0.0 copy-done
  51.4 17.2 %join.1 = (f32[64,32,128]{2,1,0:T(8,128)S(1)}, bf16[64,32,128]{2,1,0:T(8,128)(2,1)S(1)}) custom-call(s32[1]{0:T(128)} %bitcast.me_ref, bf16[8448,128]{1,0:T(8,128)(2,1)S(1)} %bitcast.7, bf16[2048,128]{1,0:T(8,128)(2,1)S(1)} %copy-done), custom_call_target="tpu_custom_call" | custom-call | tf_op jit(solution)/shard_map/join/pallas_call | solution.py:246
  68.5 0.1 collective-permute-start
  68.6 1.9 %collective-permute-done.got_ref = bf16[64,32,128]{2,1,0:T(8,128)(2,1)S(1)} collective-permute-done((bf16[64,32,128]{2,1,0:T(8,128)(2,1)S(1)}, bf16[64,32,128]{2,1,0:T(8,128)(2,1)S(1)}, u32[]{:S(2)}, u32[]{:S(2)}) %collective-permute-start) | collective-permute-done | bytes 524320 | tf_op jit(solution)/shard_map/ppermute | solution.py:371
  70.5 0.3 merge.1
  70.8 18.9 %all_to_all.11.got_ref = bf16[64,48,128]{2,1,0:T(8,128)(2,1)S(1)} all-to-all(bf16[64,48,128]{2,1,0:T(8,128)(2,1)S(1)} %merge.1), channel_id=1, replica_groups=mesh['section'=4,'dom_0'=4,'dom_1'=4,'dom_2'=2] {'section','dom_0','dom_1'}, dimensions={0} | all-to-all | bytes 1572864 | tf_op jit(solution)/shard_map/all_to_all | solution.py:372
  89.8 0.7 total.1
  90.5 2.3 %collective-permute-start.1 = (f32[16,128]{1,0:T(8,128)S(1)}, f32[16,128]{1,0:T(8,128)S(1)}, u32[]{:S(2)}, u32[]{:S(2)}) collective-permute-start(f32[16,128]{1,0:T(8,128)S(1)} %get-tuple-element.13.a_ref), channel_id=1, source_target_pairs={{0,1},{1,0},{2,3},{3,2},{4,5},{5,4},{6,7},{7,6},{8,9},{9,8},{10,11... | collective-permute-start | bytes 24584 | tf_op jit(solution)/shard_map/ppermute | solution.py:374
  92.8 0.8 collective-permute-done.1.b_ref
  93.6 2.0 %leaders.1 = f32[1,16]{1,0:T(1,128)} custom-call(f32[16,128]{1,0:T(8,128)S(1)} %get-tuple-element.13.a_ref, f32[16,128]{1,0:T(8,128)S(1)} %collective-permute-done.1.b_ref), custom_call_target="tpu_custom_call" | custom-call | tf_op jit(solution)/shard_map/leaders/pallas_call | solution.py:338
Async XLA Ops:
  8.9 42.4 %copy-start = (bf16[2048,128]{1,0:T(8,128)(2,1)S(1)}, bf16[2048,128]{1,0:T(8,128)(2,1)}, u32[]{:S(2)}) copy-start(bf16[2048,128]{1,0:T(8,128)(2,1)} %table_ref.1) | copy-start | bytes 1572868
  68.5 2.0 %collective-permute-start = (bf16[64,32,128]{2,1,0:T(8,128)(2,1)S(1)}, bf16[64,32,128]{2,1,0:T(8,128)(2,1)S(1)}, u32[]{:S(2)}, u32[]{:S(2)}) collective-permute-start(bf16[64,32,128]{2,1,0:T(8,128)(2,1)S(1)} %get-tuple-element.11), channel_id=1, source_target_pairs={{0,1},{1,0},{2,3},{3,2},{4,5},{5,4},{6,7},{7,6},{8,9},{9,8},{10,11... | collective-permute-start | bytes 1572872 | tf_op jit(solution)/shard_map/ppermute | solution.py:371
  90.5 3.1 %collective-permute-start.1 = (f32[16,128]{1,0:T(8,128)S(1)}, f32[16,128]{1,0:T(8,128)S(1)}, u32[]{:S(2)}, u32[]{:S(2)}) collective-permute-start(f32[16,128]{1,0:T(8,128)S(1)} %get-tuple-element.13.a_ref), channel_id=1, source_target_pairs={{0,1},{1,0},{2,3},{3,2},{4,5},{5,4},{6,7},{7,6},{8,9},{9,8},{10,11... | collective-permute-start | bytes 24584 | tf_op jit(solution)/shard_map/ppermute | solution.py:374

commit v4 on v2

--- a/solution.py
+++ b/solution.py
@@ -9,8 +9,9 @@
 BLOCK = 128
 TOPK = 16
 SLOTS = 64
-AREA = 72
 DESTS = 128
+AREA = 66
+FLAT = DESTS * AREA
 PIECES = 4
 BF = jnp.bfloat16
 F32 = jnp.float32
@@ -38,10 +39,10 @@
         load.start()
 
     def clear(i, _):
-        area_ref[pl.ds(pl.multiple_of(i * AREA, 8), AREA), :] = jnp.zeros((AREA, BLOCK), F32)
+        area_ref[pl.ds(pl.multiple_of(i * 64, 64), 64), :] = jnp.zeros((64, BLOCK), F32)
         return 0
 
-    lax.fori_loop(0, DESTS, clear, 0, unroll=4)
+    lax.fori_loop(0, FLAT // 64, clear, 0, unroll=4)
     for load in loads[:-1]:
         load.wait()
     lane = lax.broadcasted_iota(I32, (1, BLOCK), 1)
@@ -73,7 +74,7 @@
         counts = jnp.dot(names16, count_of, preferred_element_type=F32)
         slot = jnp.sum(names * (counts[:, :wide] + carry), axis=0, keepdims=True).astype(I32)
         carry = carry + counts[:, wide:]
-        place = jnp.where(ok, target * AREA + slot, DESTS * AREA)
+        place = jnp.where(ok, target * AREA + slot, FLAT)
         place_ref[2 * step : 2 * step + 1, :] = place[:, :BLOCK]
         place_ref[2 * step + 1 : 2 * step + 2, :] = place[:, BLOCK:]
         mine = slot_ids == slot
@@ -102,18 +103,16 @@
     lax.fori_loop(0, rows // BLOCK, put, 0)
 
     def give(i, _):
-        area16_ref[i] = area_ref[pl.ds(pl.multiple_of(i * AREA, 8), AREA), :].astype(BF)
+        at = pl.ds(pl.multiple_of(i * 64, 64), 64)
+        area16_ref[at, :] = area_ref[at, :].astype(BF)
         return 0
 
     stores = []
+    part = FLAT // PIECES
     for n in range(PIECES):
-        part = DESTS // PIECES
-        lax.fori_loop(n * part, (n + 1) * part, give, 0, unroll=4)
-        stores.append(
-            pltpu.make_async_copy(
-                area16_ref.at[pl.ds(n * part, part)], out_hbm.at[pl.ds(n * part, part)], sems.at[8 + n]
-            )
-        )
+        lax.fori_loop(n * part // 64, (n + 1) * part // 64, give, 0, unroll=3)
+        at = pl.ds(n * part, part)
+        stores.append(pltpu.make_async_copy(area16_ref.at[at], out_hbm.at[at], sems.at[8 + n]))
         stores[-1].start()
     for store in stores:
         store.wait()
@@ -124,7 +123,7 @@
     blocks = rows // BLOCK
     return pl.pallas_call(
         pack_kernel,
-        out_shape=jax.ShapeDtypeStruct((DESTS, AREA, BLOCK), BF),
+        out_shape=jax.ShapeDtypeStruct((FLAT, BLOCK), BF),
         in_specs=[HBM] * 7,
         out_specs=HBM,
         scratch_shapes=[
@@ -135,8 +134,8 @@
             pltpu.VMEM((blocks, BLOCK), I32),
             pltpu.VMEM((blocks, BLOCK), I32),
             pltpu.VMEM((blocks, BLOCK), I32),
-            pltpu.VMEM((DESTS * AREA + 8, BLOCK), F32),
-            pltpu.VMEM((DESTS, AREA, BLOCK), BF),
+            pltpu.VMEM((FLAT + 8, BLOCK), F32),
+            pltpu.VMEM((FLAT, BLOCK), BF),
             pltpu.VMEM((blocks, BLOCK), I32),
             pltpu.SMEM((blocks, BLOCK), I32),
             pltpu.SemaphoreType.DMA((8 + PIECES,)),
@@ -146,12 +145,13 @@
     )(bounds, lengths, measures, preds, dest, keys, groups)
 
 
-def join_kernel(me_ref, got_ref, table_ref, own_ref, other_ref, pair_ref, sums_ref, keyt_ref, group_ref):
-    chips = got_ref.shape[0] // 2
-    first = got_ref[:chips, SLOTS : SLOTS + 8, :].astype(F32)
-    second = got_ref[chips:, SLOTS : SLOTS + 8, :].astype(F32)
-    ka, kb = first[:, 0, :], second[:, 0, :]
-    ga, gb = first[:, 1, :], second[:, 1, :]
+def join_kernel(me_ref, got_ref, table_ref, own_ref, other_ref, pair_ref, sums_ref, keyt_ref, group_ref, aux_ref):
+    chips = DESTS // 2
+    for d in range(DESTS):
+        pair = got_ref[d * AREA + SLOTS : (d + 1) * AREA, :].astype(F32)
+        aux_ref[:, d : d + 1, :] = pair.reshape(2, 1, BLOCK)
+    ka, kb = aux_ref[0, :chips, :], aux_ref[0, chips:, :]
+    ga, gb = aux_ref[1, :chips, :], aux_ref[1, chips:, :]
 
     def halves(a, b):
         return (
@@ -180,7 +180,10 @@
             cols.append(jnp.where(ids == k, one, zero))
         found = jnp.dot(jnp.concatenate(cols, axis=1), tab, preferred_element_type=F32)
         row = jnp.where(upper, found[:, BLOCK:], found[:, :BLOCK])
-        pay = jnp.concatenate([got_ref[p, :SLOTS, :], got_ref[chips + p, :SLOTS, :]], axis=0)
+        low, high_at = p * AREA, (chips + p) * AREA
+        pay = jnp.concatenate(
+            [got_ref[low : low + SLOTS, :], got_ref[high_at : high_at + SLOTS, :]], axis=0
+        )
         joined = pay.astype(F32) * row
         high = top >= 8.0
         none = jnp.zeros_like(joined)
@@ -218,7 +221,7 @@
 
 
 def join(me, got, table):
-    chips = got.shape[0] // 2
+    chips = DESTS // 2
     return pl.pallas_call(
         join_kernel,
         out_shape=(
@@ -232,6 +235,7 @@
             pltpu.VMEM((2048, 2 * BLOCK), F32),
             pltpu.VMEM((BLOCK, BLOCK), F32),
             pltpu.VMEM((2, chips, BLOCK), F32),
+            pltpu.VMEM((2, DESTS, BLOCK), F32),
         ],
         compiler_params=pltpu.CompilerParams(vmem_limit_bytes=40 << 20),
         name="join",
@@ -335,7 +339,9 @@
     packets = pack(
         bounds, lengths, measures, pred_columns, lanes(destination), lanes(key_offset), lanes(group_ids)
     )
-    got = lax.all_to_all(packets, DEVICES, split_axis=0, concat_axis=0, tiled=True)
+    got = lax.all_to_all(
+        packets.reshape(DESTS, AREA // 2, 2, BLOCK), DEVICES, split_axis=0, concat_axis=0, tiled=True
+    ).reshape(FLAT, BLOCK)
     mine, theirs = join(me, got, build_table)
     pair = merge(mine, lax.ppermute(theirs, CORE, SWAP))
     arrived = lax.all_to_all(pair, CHIPS, split_axis=0, concat_axis=0, tiled=True)

time: 95.9 us -> 94.3 us (0.983)
  blocking collectives: 63.3 us -> 61.2 us
    all_to_all x1, blocking collectives: 44.5 us -> 42.4 us  [on_device(): lax.all_to_all(packets.reshape(DESTS, AREA // 2, 2, BLOCK), DEVICES, spli...]
where the time goes in v4:
time: 94.3 us; the launch traced here: 94.1 us
  blocking collectives  61.2 us (65%)
  Pallas kernels  26.2 us (28%)
  starting transfers between devices  3.64 us (4%)
  waiting for transfers between devices  2.37 us (3%)
    all_to_all x1, blocking collectives, on_device(): lax.all_to_all(packets.reshape(DESTS, AREA // 2, 2, BLOCK), DEVICES, spli...  42.4 us
    all_to_all x1, blocking collectives, on_device(): lax.all_to_all(pair, CHIPS, split_axis=0, concat_axis=0, tiled=True)  18.8 us
    pallas_call x1, Pallas kernels, join(): pl.pallas_call(join_kernel, out_shape=(jax.ShapeDtypeStruct((chips, 32, B...  14.9 us
    pallas_call x1, Pallas kernels, pack(): pl.pallas_call(pack_kernel, out_shape=jax.ShapeDtypeStruct((FLAT, BLOCK),...  8.3 us
    ppermute x1, starting transfers between devices, on_device(): top = leaders(scores, lax.ppermute(scores, CORE, SWAP))  2.3 us
    pallas_call x1, Pallas kernels, leaders(): pl.pallas_call(leaders_kernel, out_shape=jax.ShapeDtypeStruct((1, TOPK),...  1.95 us
  transfers between devices with their start and end apart: 2, of which 2 were waited for; matrix products, arithmetic and copies ran while one was open for 0% of the time, Pallas kernels for 0%

profile of v4, /device:TPU:1, one launch (start us, length us, event | category | flops | bytes accessed | tf_op | source)
XLA Modules:
  0.0 94.1 jit_solution(6495273033717826844)
XLA Ops:
  0.6 8.3 %pack.1 = bf16[8448,128]{1,0:T(8,128)(2,1)} custom-call(s32[2,2]{1,0:T(2,128)} %bounds_hbm, s32[32]{0:T(128)} %lengths_hbm.1, bf16[4096,128]{1,0:T(8,128)(2,1)} %measures_hbm.1, s32[2,4096]{1,0:T(2,128)} %preds_hbm.1, s32[32,128]{1,0:T(8,128)} %bitcast.9, s32[32,128]{1,0:T(8,128)} %bitcast.10, s32[32,128]{1,0:T(8,128)} %bitcast.11), custom_call_target="tpu_custom_call" | custom-call | tf_op jit(solution)/shard_map/pack/pallas_call | solution.py:124
  8.9 0.0 copy-start
  9.0 42.4 %all_to_all.10 = bf16[128,33,2,128]{3,2,1,0:T(2,128)(2,1)S(1)} all-to-all(bf16[128,33,2,128]{3,2,1,0:T(2,128)(2,1)} %bitcast.8), channel_id=1, replica_groups=mesh['section'=4,'dom_0'=4,'dom_1'=4,'dom_2'=2] {'section','dom_0','dom_..., dimensions={0} | all-to-all | bytes 4325376 | tf_op jit(solution)/shard_map/all_to_all | solution.py:342
  51.4 0.0 copy-done
  51.4 14.9 %join.1 = (f32[64,32,128]{2,1,0:T(8,128)S(1)}, bf16[64,32,128]{2,1,0:T(8,128)(2,1)S(1)}) custom-call(s32[1]{0:T(128)} %bitcast.me_ref, bf16[8448,128]{1,0:T(8,128)(2,1)S(1)} %bitcast.7, bf16[2048,128]{1,0:T(8,128)(2,1)S(1)} %copy-done), custom_call_target="tpu_custom_call" | custom-call | tf_op jit(solution)/shard_map/join/pallas_call | solution.py:225
  66.3 1.3 %collective-permute-start = (bf16[64,32,128]{2,1,0:T(8,128)(2,1)S(1)}, bf16[64,32,128]{2,1,0:T(8,128)(2,1)S(1)}, u32[]{:S(2)}, u32[]{:S(2)}) collective-permute-start(bf16[64,32,128]{2,1,0:T(8,128)(2,1)S(1)} %get-tuple-element.11), channel_id=1, source_target_pairs={{0,1},{1,0},{2,3},{3,2},{4,5},{5,4},{6,7},{7,6},{8,9},{9,8},{10,11... | collective-permute-start | bytes 1572872 | tf_op jit(solution)/shard_map/ppermute | solution.py:346
  67.7 1.5 %collective-permute-done.got_ref = bf16[64,32,128]{2,1,0:T(8,128)(2,1)S(1)} collective-permute-done((bf16[64,32,128]{2,1,0:T(8,128)(2,1)S(1)}, bf16[64,32,128]{2,1,0:T(8,128)(2,1)S(1)}, u32[]{:S(2)}, u32[]{:S(2)}) %collective-permute-start) | collective-permute-done | bytes 524320 | tf_op jit(solution)/shard_map/ppermute | solution.py:346
  69.2 0.3 merge.1
  69.5 18.8 %all_to_all.11.got_ref = bf16[64,48,128]{2,1,0:T(8,128)(2,1)S(1)} all-to-all(bf16[64,48,128]{2,1,0:T(8,128)(2,1)S(1)} %merge.1), channel_id=1, replica_groups=mesh['section'=4,'dom_0'=4,'dom_1'=4,'dom_2'=2] {'section','dom_0','dom_1'}, dimensions={0} | all-to-all | bytes 1572864 | tf_op jit(solution)/shard_map/all_to_all | solution.py:347
  88.3 0.7 total.1
  89.0 2.3 %collective-permute-start.1 = (f32[16,128]{1,0:T(8,128)S(1)}, f32[16,128]{1,0:T(8,128)S(1)}, u32[]{:S(2)}, u32[]{:S(2)}) collective-permute-start(f32[16,128]{1,0:T(8,128)S(1)} %get-tuple-element.13.a_ref), channel_id=1, source_target_pairs={{0,1},{1,0},{2,3},{3,2},{4,5},{5,4},{6,7},{7,6},{8,9},{9,8},{10,11... | collective-permute-start | bytes 24584 | tf_op jit(solution)/shard_map/ppermute | solution.py:349
  91.3 0.8 collective-permute-done.1.b_ref
  92.1 2.0 %leaders.1 = f32[1,16]{1,0:T(1,128)} custom-call(f32[16,128]{1,0:T(8,128)S(1)} %get-tuple-element.13.a_ref, f32[16,128]{1,0:T(8,128)S(1)} %collective-permute-done.1.b_ref), custom_call_target="tpu_custom_call" | custom-call | tf_op jit(solution)/shard_map/leaders/pallas_call | solution.py:313
Async XLA Ops:
  8.9 42.4 %copy-start = (bf16[2048,128]{1,0:T(8,128)(2,1)S(1)}, bf16[2048,128]{1,0:T(8,128)(2,1)}, u32[]{:S(2)}) copy-start(bf16[2048,128]{1,0:T(8,128)(2,1)} %table_ref.1) | copy-start | bytes 1572868
  66.3 2.9 %collective-permute-start = (bf16[64,32,128]{2,1,0:T(8,128)(2,1)S(1)}, bf16[64,32,128]{2,1,0:T(8,128)(2,1)S(1)}, u32[]{:S(2)}, u32[]{:S(2)}) collective-permute-start(bf16[64,32,128]{2,1,0:T(8,128)(2,1)S(1)} %get-tuple-element.11), channel_id=1, source_target_pairs={{0,1},{1,0},{2,3},{3,2},{4,5},{5,4},{6,7},{7,6},{8,9},{9,8},{10,11... | collective-permute-start | bytes 1572872 | tf_op jit(solution)/shard_map/ppermute | solution.py:346
  89.0 3.1 %collective-permute-start.1 = (f32[16,128]{1,0:T(8,128)S(1)}, f32[16,128]{1,0:T(8,128)S(1)}, u32[]{:S(2)}, u32[]{:S(2)}) collective-permute-start(f32[16,128]{1,0:T(8,128)S(1)} %get-tuple-element.13.a_ref), channel_id=1, source_target_pairs={{0,1},{1,0},{2,3},{3,2},{4,5},{5,4},{6,7},{7,6},{8,9},{9,8},{10,11... | collective-permute-start | bytes 24584 | tf_op jit(solution)/shard_map/ppermute | solution.py:349

commit v5 on v4

--- a/solution.py
+++ b/solution.py
@@ -13,6 +13,9 @@
 AREA = 66
 FLAT = DESTS * AREA
 PIECES = 4
+PER = 8
+TILES = 2
+FETCH = 2
 BF = jnp.bfloat16
 F32 = jnp.float32
 I32 = jnp.int32
@@ -20,6 +23,11 @@
 VMEM = pl.BlockSpec(memory_space=pltpu.VMEM)
 SMEM = pl.BlockSpec(memory_space=pltpu.SMEM)
 HBM = pl.BlockSpec(memory_space=pltpu.HBM)
+
+
+def group_code(g):
+    high = ((g >> 11) << 3) + (((g >> 5) & 1) << 2) + ((g >> 9) & 3)
+    return high, (((g >> 6) & 7) << 5) + (g & 31)
 
 
 def pack_kernel(
@@ -80,7 +88,7 @@
         mine = slot_ids == slot
         values = [
             jnp.where(mine, part.astype(F32), 0.0).astype(BF)
-            for part in (keys >> 8, keys & 255, groups >> 8, groups & 255)
+            for part in (keys >> 8, keys & 255, *group_code(groups))
         ]
         packed = packed + lax.dot_general(
             names16, jnp.concatenate(values, axis=0), NT, preferred_element_type=F32
@@ -145,101 +153,129 @@
     )(bounds, lengths, measures, preds, dest, keys, groups)
 
 
-def join_kernel(me_ref, got_ref, table_ref, own_ref, other_ref, pair_ref, sums_ref, keyt_ref, group_ref, aux_ref):
-    chips = DESTS // 2
+def add_groups(core, group_ref, pair_ref, sums_ref):
+    rows_at = lax.broadcasted_iota(I32, (256, BLOCK), 0).astype(F32).astype(BF)
+    one = jnp.ones((), BF)
+    zero = jnp.zeros((), BF)
+    first = (core * 4).astype(F32)
+    for k in range(DESTS // 2 // PER):
+        lows = []
+        for p in range(k * PER, (k + 1) * PER):
+            hi = group_ref[0, p : p + 1, :]
+            lows.append((jnp.where(hi >= 8.0, hi - 8.0, hi) - first, group_ref[1, p : p + 1, :]))
+        block = pair_ref[k * PER * BLOCK : (k + 1) * PER * BLOCK, :]
+        for t in range(0, 4, TILES):
+            tiles = []
+            for u in range(t, t + TILES):
+                cols = []
+                for hi, lo in lows:
+                    v = jnp.where(hi == float(u), lo, -1.0).astype(BF)
+                    cols.append(jnp.where(rows_at == jnp.broadcast_to(v, (256, BLOCK)), one, zero))
+                tiles.append(jnp.concatenate(cols, axis=1))
+            part = jnp.dot(jnp.concatenate(tiles, axis=0), block, preferred_element_type=F32)
+            at = pl.ds(t * 256, TILES * 256)
+            if k == 0:
+                sums_ref[at, :] = part
+            else:
+                sums_ref[at, :] = sums_ref[at, :] + part
+
+
+def join_kernel(me_ref, got_ref, table_ref, other_ref, pair_ref, group_ref, sums_ref, turned_ref, aux_ref):
+    blocks = DESTS // 2
     for d in range(DESTS):
         pair = got_ref[d * AREA + SLOTS : (d + 1) * AREA, :].astype(F32)
         aux_ref[:, d : d + 1, :] = pair.reshape(2, 1, BLOCK)
-    ka, kb = aux_ref[0, :chips, :], aux_ref[0, chips:, :]
-    ga, gb = aux_ref[1, :chips, :], aux_ref[1, chips:, :]
-
-    def halves(a, b):
+
+    def halves(n):
+        a, b = aux_ref[n, :blocks, :], aux_ref[n, blocks:, :]
         return (
             jnp.concatenate([a[:, :SLOTS], b[:, :SLOTS]], axis=1),
             jnp.concatenate([a[:, SLOTS:], b[:, SLOTS:]], axis=1),
         )
 
-    key_hi, key_lo = halves(ka, kb)
-    grp_hi, grp_lo = halves(ga, gb)
-    keyt_ref[...] = jnp.concatenate([key_hi * 256.0 + key_lo, grp_hi], axis=0).T
+    key_hi, key_lo = halves(0)
+    grp_hi, grp_lo = halves(1)
+    turned_ref[...] = jnp.concatenate([key_hi * 256.0 + key_lo, grp_hi], axis=0).T
     group_ref[0] = grp_hi
     group_ref[1] = grp_lo
     tab = jnp.concatenate([table_ref[:1024, :], table_ref[1024:, :]], axis=1)
     ids = lax.broadcasted_iota(I32, (BLOCK, 256), 1).astype(F32).astype(BF)
     one = jnp.ones((), BF)
     zero = jnp.zeros((), BF)
-    for p in range(chips):
-        key = jnp.broadcast_to(keyt_ref[:, p : p + 1], (BLOCK, BLOCK))
-        top = jnp.broadcast_to(keyt_ref[:, chips + p : chips + p + 1], (BLOCK, BLOCK))
-        upper = key >= 1024.0
-        key = jnp.where(upper, key - 1024.0, key)
-        cols = []
-        for t in range(4):
-            k = (key - 256.0 * t).astype(BF)
-            k = jnp.concatenate([k, k], axis=1)
-            cols.append(jnp.where(ids == k, one, zero))
-        found = jnp.dot(jnp.concatenate(cols, axis=1), tab, preferred_element_type=F32)
-        row = jnp.where(upper, found[:, BLOCK:], found[:, :BLOCK])
-        low, high_at = p * AREA, (chips + p) * AREA
-        pay = jnp.concatenate(
-            [got_ref[low : low + SLOTS, :], got_ref[high_at : high_at + SLOTS, :]], axis=0
-        )
-        joined = pay.astype(F32) * row
-        high = top >= 8.0
-        none = jnp.zeros_like(joined)
-        pair_ref[p * BLOCK : (p + 1) * BLOCK, :BLOCK] = jnp.where(high, none, joined).astype(BF)
-        pair_ref[p * BLOCK : (p + 1) * BLOCK, BLOCK:] = jnp.where(high, joined, none).astype(BF)
-
-    rows_at = lax.broadcasted_iota(I32, (256, BLOCK), 0).astype(F32).astype(BF)
-    per = 8
-    for k in range(chips // per):
-        low3 = []
-        for p in range(k * per, (k + 1) * per):
-            hi = group_ref[0, p : p + 1, :]
-            low3.append((jnp.where(hi >= 8.0, hi - 8.0, hi), group_ref[1, p : p + 1, :]))
-        block = pair_ref[k * per * BLOCK : (k + 1) * per * BLOCK, :]
-        for t in range(8):
+    for q in range(0, blocks, FETCH):
+        picks = []
+        uppers = []
+        for p in range(q, q + FETCH):
+            key = jnp.broadcast_to(turned_ref[:, p : p + 1], (BLOCK, BLOCK))
+            upper = key >= 1024.0
+            uppers.append(upper)
+            key = jnp.where(upper, key - 1024.0, key)
             cols = []
-            for hi, lo in low3:
-                v = jnp.where(hi == float(t), lo, -1.0).astype(BF)
-                cols.append(jnp.where(rows_at == jnp.broadcast_to(v, (256, BLOCK)), one, zero))
-            part = jnp.dot(jnp.concatenate(cols, axis=1), block, preferred_element_type=F32)
-            at = pl.ds(t * 256, 256)
-            if k == 0:
-                sums_ref[at, :] = part
-            else:
-                sums_ref[at, :] = sums_ref[at, :] + part
-
-    me = me_ref[0]
-    for i in range(64):
-        col = (i // 32) * BLOCK
-        base = (i % 32) * 64
-        mine = pl.ds(pl.multiple_of(base + me * 32, 8), 32)
-        theirs = pl.ds(pl.multiple_of(base + (1 - me) * 32, 8), 32)
-        own_ref[i] = sums_ref[mine, col : col + BLOCK]
-        other_ref[i] = sums_ref[theirs, col : col + BLOCK].astype(BF)
+            for t in range(4):
+                k = (key - 256.0 * t).astype(BF)
+                k = jnp.concatenate([k, k], axis=1)
+                cols.append(jnp.where(ids == k, one, zero))
+            picks.append(jnp.concatenate(cols, axis=1))
+        found = jnp.dot(jnp.concatenate(picks, axis=0), tab, preferred_element_type=F32)
+        for p in range(q, q + FETCH):
+            mine = found[(p - q) * BLOCK : (p - q + 1) * BLOCK, :]
+            row = jnp.where(uppers[p - q], mine[:, BLOCK:], mine[:, :BLOCK])
+            low, high_at = p * AREA, (blocks + p) * AREA
+            pay = jnp.concatenate(
+                [got_ref[low : low + SLOTS, :], got_ref[high_at : high_at + SLOTS, :]], axis=0
+            )
+            joined = pay.astype(F32) * row
+            high = jnp.broadcast_to(turned_ref[:, blocks + p : blocks + p + 1], (BLOCK, BLOCK)) >= 8.0
+            none = jnp.zeros_like(joined)
+            to = slice(p * BLOCK, (p + 1) * BLOCK)
+            pair_ref[to, :BLOCK] = jnp.where(high, none, joined).astype(BF)
+            pair_ref[to, BLOCK:] = jnp.where(high, joined, none).astype(BF)
+    add_groups(1 - me_ref[0], group_ref, pair_ref, sums_ref)
+    for q in range(64):
+        at = slice(q % 32 * 32, (q % 32 + 1) * 32)
+        other_ref[q] = sums_ref[at, q // 32 * BLOCK : (q // 32 + 1) * BLOCK].astype(BF)
 
 
 def join(me, got, table):
-    chips = DESTS // 2
+    blocks = DESTS // 2
     return pl.pallas_call(
         join_kernel,
         out_shape=(
-            jax.ShapeDtypeStruct((chips, 32, BLOCK), F32),
-            jax.ShapeDtypeStruct((chips, 32, BLOCK), BF),
+            jax.ShapeDtypeStruct((64, 32, BLOCK), BF),
+            jax.ShapeDtypeStruct((blocks * BLOCK, 2 * BLOCK), BF),
+            jax.ShapeDtypeStruct((2, blocks, BLOCK), F32),
         ),
         in_specs=[SMEM, VMEM, VMEM],
-        out_specs=(VMEM, VMEM),
+        out_specs=(VMEM, VMEM, VMEM),
         scratch_shapes=[
-            pltpu.VMEM((chips * BLOCK, 2 * BLOCK), BF),
-            pltpu.VMEM((2048, 2 * BLOCK), F32),
+            pltpu.VMEM((1024, 2 * BLOCK), F32),
             pltpu.VMEM((BLOCK, BLOCK), F32),
-            pltpu.VMEM((2, chips, BLOCK), F32),
             pltpu.VMEM((2, DESTS, BLOCK), F32),
         ],
-        compiler_params=pltpu.CompilerParams(vmem_limit_bytes=40 << 20),
+        cost_estimate=pl.CostEstimate(flops=9 << 30, bytes_accessed=8 << 20, transcendentals=0),
+        compiler_params=pltpu.CompilerParams(vmem_limit_bytes=30 << 20),
         name="join",
     )(me, got, table)
+
+
+def rest_kernel(me_ref, pair_ref, group_ref, own_ref, sums_ref):
+    add_groups(me_ref[0], group_ref, pair_ref, sums_ref)
+    for q in range(64):
+        at = slice(q % 32 * 32, (q % 32 + 1) * 32)
+        own_ref[q] = sums_ref[at, q // 32 * BLOCK : (q // 32 + 1) * BLOCK]
+
+
+def rest(me, pair, group):
+    return pl.pallas_call(
+        rest_kernel,
+        out_shape=jax.ShapeDtypeStruct((64, 32, BLOCK), F32),
+        in_specs=[SMEM, VMEM, VMEM],
+        out_specs=VMEM,
+        scratch_shapes=[pltpu.VMEM((1024, 2 * BLOCK), F32)],
+        cost_estimate=pl.CostEstimate(flops=5 << 30, bytes_accessed=8 << 20, transcendentals=0),
+        compiler_params=pltpu.CompilerParams(vmem_limit_bytes=24 << 20),
+        name="rest",
+    )(me, pair, group)
 
 
 def merge_kernel(own_ref, got_ref, out_ref):
@@ -342,8 +378,9 @@
     got = lax.all_to_all(
         packets.reshape(DESTS, AREA // 2, 2, BLOCK), DEVICES, split_axis=0, concat_axis=0, tiled=True
     ).reshape(FLAT, BLOCK)
-    mine, theirs = join(me, got, build_table)
-    pair = merge(mine, lax.ppermute(theirs, CORE, SWAP))
+    theirs, joined, codes = join(me, got, build_table)
+    from_partner = lax.ppermute(theirs, CORE, SWAP)
+    pair = merge(rest(me, joined, codes), from_partner)
     arrived = lax.all_to_all(pair, CHIPS, split_axis=0, concat_axis=0, tiled=True)
     group_sums, scores = total(arrived, 32)
     top = leaders(scores, lax.ppermute(scores, CORE, SWAP))

time: 94.3 us -> 92.3 us (0.979)
  waiting for transfers between devices: 2.37 us -> 0.83 us
    ppermute x1, waiting for transfers between devices: 1.54 us -> 0.01 us  [on_device(): from_partner = lax.ppermute(theirs, CORE, SWAP)]
    pallas_call x1 -> x2, Pallas kernels: 14.9 us -> 14.3 us  [the longest x1 9.87 us: join(): pl.pallas_call(join_kernel, out_shape=(jax.ShapeDtypeStruct((64, 32, BLOC...]
  transfers between devices with their start and end apart: 2 -> 2, of which waited for: 2 -> 1; matrix products, arithmetic and copies ran while one was open for 0% -> 0% of each run, Pallas kernels for 0% -> 5%
where the time goes in v5:
time: 92.3 us; the launch traced here: 92.1 us
  blocking collectives  61.5 us (67%)
  Pallas kernels  25.6 us (28%)
  starting transfers between devices  3.51 us (4%)
    all_to_all x1, blocking collectives, on_device(): lax.all_to_all(packets.reshape(DESTS, AREA // 2, 2, BLOCK), DEVICES, spli...  42.4 us
    all_to_all x1, blocking collectives, on_device(): lax.all_to_all(pair, CHIPS, split_axis=0, concat_axis=0, tiled=True)  19.1 us
    pallas_call x1, Pallas kernels, join(): pl.pallas_call(join_kernel, out_shape=(jax.ShapeDtypeStruct((64, 32, BLOC...  9.87 us
    pallas_call x1, Pallas kernels, pack(): pl.pallas_call(pack_kernel, out_shape=jax.ShapeDtypeStruct((FLAT, BLOCK),...  8.31 us
    pallas_call x1, Pallas kernels, rest(): pl.pallas_call(rest_kernel, out_shape=jax.ShapeDtypeStruct((64, 32, BLOCK...  4.47 us
    ppermute x1, starting transfers between devices, on_device(): top = leaders(scores, lax.ppermute(scores, CORE, SWAP))  2 us
    pallas_call x1, Pallas kernels, leaders(): pl.pallas_call(leaders_kernel, out_shape=jax.ShapeDtypeStruct((1, TOPK),...  1.95 us
  transfers between devices with their start and end apart: 2, of which 1 were waited for; matrix products, arithmetic and copies ran while one was open for 0% of the time, Pallas kernels for 5%

profile of v5, /device:TPU:1, one launch (start us, length us, event | category | flops | bytes accessed | tf_op | source)
XLA Modules:
  0.0 92.1 jit_solution(17052647210888459302)
XLA Ops:
  0.6 8.3 %pack.1 = bf16[8448,128]{1,0:T(8,128)(2,1)} custom-call(s32[2,2]{1,0:T(2,128)} %bounds_hbm, s32[32]{0:T(128)} %lengths_hbm.1, bf16[4096,128]{1,0:T(8,128)(2,1)} %measures_hbm.1, s32[2,4096]{1,0:T(2,128)} %preds_hbm.1, s32[32,128]{1,0:T(8,128)} %bitcast.9, s32[32,128]{1,0:T(8,128)} %bitcast.10, s32[32,128]{1,0:T(8,128)} %bitcast.11), custom_call_target="tpu_custom_call" | custom-call | tf_op jit(solution)/shard_map/pack/pallas_call | solution.py:132
  8.9 0.0 copy-start
  9.0 42.4 %all_to_all.10 = bf16[128,33,2,128]{3,2,1,0:T(2,128)(2,1)S(1)} all-to-all(bf16[128,33,2,128]{3,2,1,0:T(2,128)(2,1)} %bitcast.8), channel_id=1, replica_groups=mesh['section'=4,'dom_0'=4,'dom_1'=4,'dom_2'=2] {'section','dom_0','dom_..., dimensions={0} | all-to-all | bytes 4325376 | tf_op jit(solution)/shard_map/all_to_all | solution.py:378
  51.4 0.0 copy-done
  51.4 9.9 %join.1 = (bf16[64,32,128]{2,1,0:T(8,128)(2,1)S(1)}, bf16[8192,256]{1,0:T(8,128)(2,1)S(1)}, f32[2,64,128]{2,1,0:T(8,128)S(1)}) custom-call(s32[1]{0:T(128)} %bitcast.me_ref, bf16[8448,128]{1,0:T(8,128)(2,1)S(1)} %bitcast.7, bf16[2048,128]{1,0:T(8,128)(2,1)S(1)} %copy-done), custom_call_target="tpu_custom_call" | custom-call | flops 9663676416 | bytes 8388608 | tf_op jit(solution)/shard_map/join/pallas_call | solution.py:241
  61.2 1.5 %collective-permute-start = (bf16[64,32,128]{2,1,0:T(8,128)(2,1)S(1)}, bf16[64,32,128]{2,1,0:T(8,128)(2,1)S(1)}, u32[]{:S(2)}, u32[]{:S(2)}) collective-permute-start(bf16[64,32,128]{2,1,0:T(8,128)(2,1)S(1)} %get-tuple-element.13), channel_id=1, source_target_pairs={{0,1},{1,0},{2,3},{3,2},{4,5},{5,4},{6,7},{7,6},{8,9},{9,8},{10,11... | collective-permute-start | bytes 1572872 | tf_op jit(solution)/shard_map/ppermute | solution.py:382
  62.8 4.5 %rest.1.own_ref = f32[64,32,128]{2,1,0:T(8,128)S(1)} custom-call(s32[1]{0:T(128)} %bitcast.me_ref, bf16[8192,256]{1,0:T(8,128)(2,1)S(1)} %get-tuple-element.11.pair_ref, f32[2,64,128]{2,1,0:T(8,128)S(1)} %get-tuple-element.12.group_ref), custom_call_target="tpu_custom_call" | custom-call | flops 5368709120 | bytes 8388608 | tf_op jit(solution)/shard_map/rest/pallas_call | solution.py:269
  67.2 0.0 collective-permute-done.got_ref
  67.2 0.3 merge.1
  67.5 19.1 %all_to_all.11.got_ref = bf16[64,48,128]{2,1,0:T(8,128)(2,1)S(1)} all-to-all(bf16[64,48,128]{2,1,0:T(8,128)(2,1)S(1)} %merge.1), channel_id=1, replica_groups=mesh['section'=4,'dom_0'=4,'dom_1'=4,'dom_2'=2] {'section','dom_0','dom_1'}, dimensions={0} | all-to-all | bytes 1572864 | tf_op jit(solution)/shard_map/all_to_all | solution.py:384
  86.6 0.7 total.1
  87.3 2.0 %collective-permute-start.1 = (f32[16,128]{1,0:T(8,128)S(1)}, f32[16,128]{1,0:T(8,128)S(1)}, u32[]{:S(2)}, u32[]{:S(2)}) collective-permute-start(f32[16,128]{1,0:T(8,128)S(1)} %get-tuple-element.15.a_ref), channel_id=1, source_target_pairs={{0,1},{1,0},{2,3},{3,2},{4,5},{5,4},{6,7},{7,6},{8,9},{9,8},{10,11... | collective-permute-start | bytes 24584 | tf_op jit(solution)/shard_map/ppermute | solution.py:386
  89.3 0.8 collective-permute-done.1.b_ref
  90.2 2.0 %leaders.1 = f32[1,16]{1,0:T(1,128)} custom-call(f32[16,128]{1,0:T(8,128)S(1)} %get-tuple-element.15.a_ref, f32[16,128]{1,0:T(8,128)S(1)} %collective-permute-done.1.b_ref), custom_call_target="tpu_custom_call" | custom-call | tf_op jit(solution)/shard_map/leaders/pallas_call | solution.py:349
Async XLA Ops:
  8.9 42.4 %copy-start = (bf16[2048,128]{1,0:T(8,128)(2,1)S(1)}, bf16[2048,128]{1,0:T(8,128)(2,1)}, u32[]{:S(2)}) copy-start(bf16[2048,128]{1,0:T(8,128)(2,1)} %table_ref.1) | copy-start | bytes 1572868
  61.2 6.0 %collective-permute-start = (bf16[64,32,128]{2,1,0:T(8,128)(2,1)S(1)}, bf16[64,32,128]{2,1,0:T(8,128)(2,1)S(1)}, u32[]{:S(2)}, u32[]{:S(2)}) collective-permute-start(bf16[64,32,128]{2,1,0:T(8,128)(2,1)S(1)} %get-tuple-element.13), channel_id=1, source_target_pairs={{0,1},{1,0},{2,3},{3,2},{4,5},{5,4},{6,7},{7,6},{8,9},{9,8},{10,11... | collective-permute-start | bytes 1572872 | tf_op jit(solution)/shard_map/ppermute | solution.py:382
  87.3 2.8 %collective-permute-start.1 = (f32[16,128]{1,0:T(8,128)S(1)}, f32[16,128]{1,0:T(8,128)S(1)}, u32[]{:S(2)}, u32[]{:S(2)}) collective-permute-start(f32[16,128]{1,0:T(8,128)S(1)} %get-tuple-element.15.a_ref), channel_id=1, source_target_pairs={{0,1},{1,0},{2,3},{3,2},{4,5},{5,4},{6,7},{7,6},{8,9},{9,8},{10,11... | collective-permute-start | bytes 24584 | tf_op jit(solution)/shard_map/ppermute | solution.py:386

commit v6 on v5

--- a/solution.py
+++ b/solution.py
@@ -33,7 +33,7 @@
 def pack_kernel(
     bounds_hbm, lengths_hbm, measures_hbm, preds_hbm, dest_hbm, keys_hbm, groups_hbm, out_hbm,
     bounds_ref, lengths_ref, measures_ref, preds_ref, dest_ref, keys_ref, groups_ref,
-    area_ref, area16_ref, place_ref, place_smem, sems,
+    area_ref, area16_ref, names_ref, values_ref, place_ref, place_smem, sems,
 ):
     rows = measures_ref.shape[0]
     wide = 2 * BLOCK
@@ -57,11 +57,12 @@
     before = (
         lax.broadcasted_iota(I32, (wide, wide), 0) < lax.broadcasted_iota(I32, (wide, wide), 1)
     ).astype(F32).astype(BF)
-    count_of = jnp.concatenate([before, jnp.ones((wide, wide), BF)], axis=1)
+    count_of = jnp.concatenate([before, jnp.ones((wide, BLOCK), BF)], axis=1)
     dest_ids = lax.broadcasted_iota(I32, (DESTS, wide), 0)
     slot_ids = lax.broadcasted_iota(I32, (SLOTS, wide), 0)
-    carry = jnp.zeros((DESTS, wide), F32)
-    packed = jnp.zeros((DESTS, 4 * SLOTS), F32)
+    carry = jnp.zeros((DESTS, BLOCK), F32)
+    blocks = rows // BLOCK
+    places = []
 
     def pair(ref, step):
         return jnp.concatenate(
@@ -77,10 +78,11 @@
         target = jnp.where(ok, pair(dest_ref, step), -1)
         keys = pair(keys_ref, step)
         groups = pair(groups_ref, step)
-        names = (dest_ids == target).astype(F32)
-        names16 = names.astype(BF)
-        counts = jnp.dot(names16, count_of, preferred_element_type=F32)
-        slot = jnp.sum(names * (counts[:, :wide] + carry), axis=0, keepdims=True).astype(I32)
+        hit = dest_ids == target
+        names = hit.astype(F32).astype(BF)
+        counts = jnp.dot(names, count_of, preferred_element_type=F32)
+        prior = counts[:, :wide] + jnp.concatenate([carry, carry], axis=1)
+        slot = jnp.sum(jnp.where(hit, prior, 0.0), axis=0, keepdims=True).astype(I32)
         carry = carry + counts[:, wide:]
         place = jnp.where(ok, target * AREA + slot, FLAT)
         place_ref[2 * step : 2 * step + 1, :] = place[:, :BLOCK]
@@ -90,16 +92,22 @@
             jnp.where(mine, part.astype(F32), 0.0).astype(BF)
             for part in (keys >> 8, keys & 255, *group_code(groups))
         ]
-        packed = packed + lax.dot_general(
-            names16, jnp.concatenate(values, axis=0), NT, preferred_element_type=F32
-        )
-    copy = pltpu.make_async_copy(place_ref, place_smem, sems.at[len(loads)])
-    copy.start()
+        names_ref[:, at] = names
+        values_ref[:, at] = jnp.concatenate(values, axis=0)
+        done = (step + 1) * 2
+        if done % (blocks // 2) == 0:
+            part = pl.ds(done - blocks // 2, blocks // 2)
+            places.append(
+                pltpu.make_async_copy(
+                    place_ref.at[part], place_smem.at[part], sems.at[len(loads) + len(places)]
+                )
+            )
+            places[-1].start()
+    packed = lax.dot_general(names_ref[...], values_ref[...], NT, preferred_element_type=F32)
     for d in range(DESTS):
         area_ref[d * AREA + SLOTS : d * AREA + SLOTS + 1, :] = packed[d : d + 1, :BLOCK]
         area_ref[d * AREA + SLOTS + 1 : d * AREA + SLOTS + 2, :] = packed[d : d + 1, BLOCK:]
     loads[-1].wait()
-    copy.wait()
 
     def put(b, _):
         for k in range(BLOCK // 16):
@@ -108,7 +116,9 @@
                 area_ref[pl.ds(place_smem[b, k * 16 + u], 1), :] = x[u : u + 1, :]
         return 0
 
-    lax.fori_loop(0, rows // BLOCK, put, 0)
+    for n, copy in enumerate(places):
+        copy.wait()
+        lax.fori_loop(n * blocks // 2, (n + 1) * blocks // 2, put, 0)
 
     def give(i, _):
         at = pl.ds(pl.multiple_of(i * 64, 64), 64)
@@ -120,7 +130,7 @@
     for n in range(PIECES):
         lax.fori_loop(n * part // 64, (n + 1) * part // 64, give, 0, unroll=3)
         at = pl.ds(n * part, part)
-        stores.append(pltpu.make_async_copy(area16_ref.at[at], out_hbm.at[at], sems.at[8 + n]))
+        stores.append(pltpu.make_async_copy(area16_ref.at[at], out_hbm.at[at], sems.at[9 + n]))
         stores[-1].start()
     for store in stores:
         store.wait()
@@ -144,9 +154,11 @@
             pltpu.VMEM((blocks, BLOCK), I32),
             pltpu.VMEM((FLAT + 8, BLOCK), F32),
             pltpu.VMEM((FLAT, BLOCK), BF),
+            pltpu.VMEM((DESTS, rows), BF),
+            pltpu.VMEM((4 * SLOTS, rows), BF),
             pltpu.VMEM((blocks, BLOCK), I32),
             pltpu.SMEM((blocks, BLOCK), I32),
-            pltpu.SemaphoreType.DMA((8 + PIECES,)),
+            pltpu.SemaphoreType.DMA((9 + PIECES,)),
         ],
         compiler_params=pltpu.CompilerParams(vmem_limit_bytes=58 << 20),
         name="pack",
@@ -327,7 +339,9 @@
     )(got)
 
 
-def leaders_kernel(a_ref, b_ref, out_ref):
+def leaders_kernel(sums_ref, a_ref, b_ref, sums_hbm, out_ref, sem):
+    copy = pltpu.make_async_copy(sums_ref, sums_hbm, sem)
+    copy.start()
     x = jnp.concatenate([a_ref[...], b_ref[...]], axis=0)
     lane = lax.broadcasted_iota(I32, (1, BLOCK), 1)
     taken = jnp.zeros((1, 1), F32)
@@ -343,17 +357,22 @@
         taken = taken + count
         x = jnp.where(same, -jnp.inf, x)
     out_ref[...] = out[:, :TOPK]
-
-
-def leaders(a, b):
+    copy.wait()
+
+
+def leaders(sums, a, b):
     return pl.pallas_call(
         leaders_kernel,
-        out_shape=jax.ShapeDtypeStruct((1, TOPK), F32),
-        in_specs=[VMEM, VMEM],
-        out_specs=VMEM,
+        out_shape=(
+            jax.ShapeDtypeStruct(sums.shape, F32),
+            jax.ShapeDtypeStruct((1, TOPK), F32),
+        ),
+        in_specs=[VMEM, VMEM, VMEM],
+        out_specs=(HBM, VMEM),
+        scratch_shapes=[pltpu.SemaphoreType.DMA],
         compiler_params=pltpu.CompilerParams(vmem_limit_bytes=4 << 20),
         name="leaders",
-    )(a, b)
+    )(sums, a, b)
 
 
 CHIPS = ("section", "dom_0", "dom_1")
@@ -383,7 +402,7 @@
     pair = merge(rest(me, joined, codes), from_partner)
     arrived = lax.all_to_all(pair, CHIPS, split_axis=0, concat_axis=0, tiled=True)
     group_sums, scores = total(arrived, 32)
-    top = leaders(scores, lax.ppermute(scores, CORE, SWAP))
+    group_sums, top = leaders(group_sums, scores, lax.ppermute(scores, CORE, SWAP))
     return group_sums, top.reshape(TOPK)
 
 

time: 92.3 us -> 91.2 us (0.988)
  Pallas kernels: 25.6 us -> 24.2 us
where the time goes in v6:
time: 91.2 us; the launch traced here: 91 us
  blocking collectives  61.5 us (67%)
  Pallas kernels  24.2 us (27%)
  starting transfers between devices  3.6 us (4%)
    all_to_all x1, blocking collectives, on_device(): lax.all_to_all(packets.reshape(DESTS, AREA // 2, 2, BLOCK), DEVICES, spli...  42.4 us
    all_to_all x1, blocking collectives, on_device(): lax.all_to_all(pair, CHIPS, split_axis=0, concat_axis=0, tiled=True)  19.1 us
    pallas_call x1, Pallas kernels, join(): pl.pallas_call(join_kernel, out_shape=(jax.ShapeDtypeStruct((64, 32, BLOC...  9.87 us
    pallas_call x1, Pallas kernels, pack(): pl.pallas_call(pack_kernel, out_shape=jax.ShapeDtypeStruct((FLAT, BLOCK),...  7.47 us
    pallas_call x1, Pallas kernels, rest(): pl.pallas_call(rest_kernel, out_shape=jax.ShapeDtypeStruct((64, 32, BLOCK...  4.47 us
    ppermute x1, starting transfers between devices, on_device(): lax.ppermute(scores, CORE, SWAP)  2.08 us
    pallas_call x1, Pallas kernels, leaders(): pl.pallas_call(leaders_kernel, out_shape=(jax.ShapeDtypeStruct(sums.shape...  1.96 us
  transfers between devices with their start and end apart: 2, of which 1 were waited for; matrix products, arithmetic and copies ran while one was open for 0% of the time, Pallas kernels for 5%

profile of v6, /device:TPU:1, one launch (start us, length us, event | category | flops | bytes accessed | tf_op | source)
XLA Modules:
  0.0 91.0 jit_solution(14657159543979283598)
XLA Ops:
  0.6 7.5 %pack.1 = bf16[8448,128]{1,0:T(8,128)(2,1)} custom-call(s32[2,2]{1,0:T(2,128)} %bounds_hbm, s32[32]{0:T(128)} %lengths_hbm.1, bf16[4096,128]{1,0:T(8,128)(2,1)} %measures_hbm.1, s32[2,4096]{1,0:T(2,128)} %preds_hbm.1, s32[32,128]{1,0:T(8,128)} %bitcast.9, s32[32,128]{1,0:T(8,128)} %bitcast.10, s32[32,128]{1,0:T(8,128)} %bitcast.11), custom_call_target="tpu_custom_call" | custom-call | tf_op jit(solution)/shard_map/pack/pallas_call | solution.py:142
  8.1 0.0 copy-start
  8.1 42.4 %all_to_all.10 = bf16[128,33,2,128]{3,2,1,0:T(2,128)(2,1)S(1)} all-to-all(bf16[128,33,2,128]{3,2,1,0:T(2,128)(2,1)} %bitcast.8), channel_id=1, replica_groups=mesh['section'=4,'dom_0'=4,'dom_1'=4,'dom_2'=2] {'section','dom_0','dom_..., dimensions={0} | all-to-all | bytes 4325376 | tf_op jit(solution)/shard_map/all_to_all | solution.py:397
  50.5 0.0 copy-done
  50.5 9.9 %join.1 = (bf16[64,32,128]{2,1,0:T(8,128)(2,1)S(1)}, bf16[8192,256]{1,0:T(8,128)(2,1)S(1)}, f32[2,64,128]{2,1,0:T(8,128)S(1)}) custom-call(s32[1]{0:T(128)} %bitcast.me_ref, bf16[8448,128]{1,0:T(8,128)(2,1)S(1)} %bitcast.7, bf16[2048,128]{1,0:T(8,128)(2,1)S(1)} %copy-done), custom_call_target="tpu_custom_call" | custom-call | flops 9663676416 | bytes 8388608 | tf_op jit(solution)/shard_map/join/pallas_call | solution.py:253
  60.4 1.5 %collective-permute-start = (bf16[64,32,128]{2,1,0:T(8,128)(2,1)S(1)}, bf16[64,32,128]{2,1,0:T(8,128)(2,1)S(1)}, u32[]{:S(2)}, u32[]{:S(2)}) collective-permute-start(bf16[64,32,128]{2,1,0:T(8,128)(2,1)S(1)} %get-tuple-element.15), channel_id=1, source_target_pairs={{0,1},{1,0},{2,3},{3,2},{4,5},{5,4},{6,7},{7,6},{8,9},{9,8},{10,11... | collective-permute-start | bytes 1572872 | tf_op jit(solution)/shard_map/ppermute | solution.py:401
  61.9 4.5 %rest.1.own_ref = f32[64,32,128]{2,1,0:T(8,128)S(1)} custom-call(s32[1]{0:T(128)} %bitcast.me_ref, bf16[8192,256]{1,0:T(8,128)(2,1)S(1)} %get-tuple-element.13.pair_ref, f32[2,64,128]{2,1,0:T(8,128)S(1)} %get-tuple-element.14.group_ref), custom_call_target="tpu_custom_call" | custom-call | flops 5368709120 | bytes 8388608 | tf_op jit(solution)/shard_map/rest/pallas_call | solution.py:281
  66.4 0.0 collective-permute-done.got_ref
  66.4 0.3 merge.1
  66.7 19.1 %all_to_all.11.got_ref = bf16[64,48,128]{2,1,0:T(8,128)(2,1)S(1)} all-to-all(bf16[64,48,128]{2,1,0:T(8,128)(2,1)S(1)} %merge.1), channel_id=1, replica_groups=mesh['section'=4,'dom_0'=4,'dom_1'=4,'dom_2'=2] {'section','dom_0','dom_1'}, dimensions={0} | all-to-all | bytes 1572864 | tf_op jit(solution)/shard_map/all_to_all | solution.py:403
  85.8 0.1 total.1
  85.9 2.1 %collective-permute-start.1 = (f32[16,128]{1,0:T(8,128)S(1)}, f32[16,128]{1,0:T(8,128)S(1)}, u32[]{:S(2)}, u32[]{:S(2)}) collective-permute-start(f32[16,128]{1,0:T(8,128)S(1)} %get-tuple-element.17.a_ref), channel_id=1, source_target_pairs={{0,1},{1,0},{2,3},{3,2},{4,5},{5,4},{6,7},{7,6},{8,9},{9,8},{10,11... | collective-permute-start | bytes 24584 | tf_op jit(solution)/shard_map/ppermute | solution.py:405
  88.0 0.8 collective-permute-done.1.b_ref
  88.8 2.0 %leaders.1 = (f32[32,128]{1,0:T(8,128)}, f32[1,16]{1,0:T(1,128)}) custom-call(f32[32,128]{1,0:T(8,128)S(1)} %get-tuple-element.16.sums_ref, f32[16,128]{1,0:T(8,128)S(1)} %get-tuple-element.17.a_ref, f32[16,128]{1,0:T(8,128)S(1)} %collective-permute-done.1.b_ref), custom_call_target="tpu_custom_call" | custom-call | tf_op jit(solution)/shard_map/leaders/pallas_call | solution.py:364
Async XLA Ops:
  8.1 42.4 %copy-start = (bf16[2048,128]{1,0:T(8,128)(2,1)S(1)}, bf16[2048,128]{1,0:T(8,128)(2,1)}, u32[]{:S(2)}) copy-start(bf16[2048,128]{1,0:T(8,128)(2,1)} %table_ref.1) | copy-start | bytes 1572868
  60.4 6.0 %collective-permute-start = (bf16[64,32,128]{2,1,0:T(8,128)(2,1)S(1)}, bf16[64,32,128]{2,1,0:T(8,128)(2,1)S(1)}, u32[]{:S(2)}, u32[]{:S(2)}) collective-permute-start(bf16[64,32,128]{2,1,0:T(8,128)(2,1)S(1)} %get-tuple-element.15), channel_id=1, source_target_pairs={{0,1},{1,0},{2,3},{3,2},{4,5},{5,4},{6,7},{7,6},{8,9},{9,8},{10,11... | collective-permute-start | bytes 1572872 | tf_op jit(solution)/shard_map/ppermute | solution.py:401
  85.9 2.9 %collective-permute-start.1 = (f32[16,128]{1,0:T(8,128)S(1)}, f32[16,128]{1,0:T(8,128)S(1)}, u32[]{:S(2)}, u32[]{:S(2)}) collective-permute-start(f32[16,128]{1,0:T(8,128)S(1)} %get-tuple-element.17.a_ref), channel_id=1, source_target_pairs={{0,1},{1,0},{2,3},{3,2},{4,5},{5,4},{6,7},{7,6},{8,9},{9,8},{10,11... | collective-permute-start | bytes 24584 | tf_op jit(solution)/shard_map/ppermute | solution.py:405

commit v7 on v6

--- a/solution.py
+++ b/solution.py
@@ -109,16 +109,14 @@
         area_ref[d * AREA + SLOTS + 1 : d * AREA + SLOTS + 2, :] = packed[d : d + 1, BLOCK:]
     loads[-1].wait()
 
-    def put(b, _):
-        for k in range(BLOCK // 16):
-            x = measures_ref[pl.ds(pl.multiple_of(b * BLOCK + k * 16, 16), 16), :].astype(F32)
-            for u in range(16):
-                area_ref[pl.ds(place_smem[b, k * 16 + u], 1), :] = x[u : u + 1, :]
-        return 0
-
     for n, copy in enumerate(places):
         copy.wait()
-        lax.fori_loop(n * blocks // 2, (n + 1) * blocks // 2, put, 0)
+        for b in range(n * blocks // 2, (n + 1) * blocks // 2):
+            for k in range(BLOCK // 16):
+                first = b * BLOCK + k * 16
+                x = measures_ref[first : first + 16, :].astype(F32)
+                for u in range(16):
+                    area_ref[pl.ds(place_smem[b, k * 16 + u], 1), :] = x[u : u + 1, :]
 
     def give(i, _):
         at = pl.ds(pl.multiple_of(i * 64, 64), 64)
@@ -343,19 +341,41 @@
     copy = pltpu.make_async_copy(sums_ref, sums_hbm, sem)
     copy.start()
     x = jnp.concatenate([a_ref[...], b_ref[...]], axis=0)
-    lane = lax.broadcasted_iota(I32, (1, BLOCK), 1)
-    taken = jnp.zeros((1, 1), F32)
-    out = jnp.full((1, BLOCK), -jnp.inf, F32)
-    place = lane.astype(F32)
-    for _ in range(TOPK):
-        best = jnp.max(jnp.max(x, axis=0, keepdims=True), axis=1, keepdims=True)
-        same = x == best
-        count = jnp.sum(
-            jnp.sum(same.astype(F32), axis=0, keepdims=True), axis=1, keepdims=True
-        )
-        out = jnp.where((place >= taken) & (place < taken + count), best, out)
-        taken = taken + count
-        x = jnp.where(same, -jnp.inf, x)
+    lanes = 4 * BLOCK
+
+    def ids(shape, dim):
+        return lax.broadcasted_iota(I32, shape, dim)
+
+    def column(v):
+        return jnp.broadcast_to(v, (BLOCK, BLOCK)).T
+
+    best = jnp.max(x, axis=0, keepdims=True)
+    down = column(best)
+    square = (BLOCK, BLOCK)
+    over = (down > best) | ((down == best) & (ids(square, 0) < ids(square, 1)))
+    rank = jnp.sum(over.astype(F32), axis=0, keepdims=True).astype(I32)
+    pick = (ids((TOPK, BLOCK), 0) == rank).astype(F32)
+    found = lax.dot_general(
+        pick, x, NT, precision=lax.Precision.HIGHEST, preferred_element_type=F32
+    )
+    spread = (ids((x.shape[0], lanes), 0) == ids((x.shape[0], lanes), 1) % x.shape[0]).astype(F32)
+    tiled = jnp.dot(found, spread, precision=lax.Precision.HIGHEST, preferred_element_type=F32)
+    keep = ids((TOPK, lanes), 0) == ids((TOPK, lanes), 1) // x.shape[0]
+    flat = jnp.sum(jnp.where(keep, tiled, 0.0), axis=0, keepdims=True)
+    pieces = [flat[:, n * BLOCK : (n + 1) * BLOCK] for n in range(4)]
+    out = jnp.zeros((1, BLOCK), F32)
+    for m in range(4):
+        down = column(pieces[m])
+        wins = jnp.zeros(square, F32)
+        for n in range(4):
+            over = pieces[n] > down
+            if n < m:
+                over = over | (pieces[n] == down)
+            elif n == m:
+                over = over | ((pieces[n] == down) & (ids(square, 1) < ids(square, 0)))
+            wins = wins + over.astype(F32)
+        place = jnp.sum(wins, axis=1, keepdims=True).astype(I32)
+        out = out + jnp.sum(jnp.where(place == ids(square, 1), down, 0.0), axis=0, keepdims=True)
     out_ref[...] = out[:, :TOPK]
     copy.wait()
 

time: 91.2 us -> 88.9 us (0.975)
  Pallas kernels: 24.2 us -> 22.1 us
    pallas_call x1, Pallas kernels: 7.47 us -> 6.1 us  [pack(): pl.pallas_call(pack_kernel, out_shape=jax.ShapeDtypeStruct((FLAT, BLOCK),...]
where the time goes in v7:
time: 88.9 us; the launch traced here: 88.7 us
  blocking collectives  61.5 us (69%)
  Pallas kernels  22.1 us (25%)
  starting transfers between devices  3.41 us (4%)
    all_to_all x1, blocking collectives, on_device(): lax.all_to_all(packets.reshape(DESTS, AREA // 2, 2, BLOCK), DEVICES, spli...  42.4 us
    all_to_all x1, blocking collectives, on_device(): lax.all_to_all(pair, CHIPS, split_axis=0, concat_axis=0, tiled=True)  19.1 us
    pallas_call x1, Pallas kernels, join(): pl.pallas_call(join_kernel, out_shape=(jax.ShapeDtypeStruct((64, 32, BLOC...  9.87 us
    pallas_call x1, Pallas kernels, pack(): pl.pallas_call(pack_kernel, out_shape=jax.ShapeDtypeStruct((FLAT, BLOCK),...  6.1 us
    pallas_call x1, Pallas kernels, rest(): pl.pallas_call(rest_kernel, out_shape=jax.ShapeDtypeStruct((64, 32, BLOCK...  4.47 us
    ppermute x1, starting transfers between devices, on_device(): lax.ppermute(scores, CORE, SWAP)  2.08 us
  transfers between devices with their start and end apart: 2, of which 1 were waited for; matrix products, arithmetic and copies ran while one was open for 0% of the time, Pallas kernels for 5%

profile of v7, /device:TPU:1, one launch (start us, length us, event | category | flops | bytes accessed | tf_op | source)
XLA Modules:
  0.0 88.7 jit_solution(13444711066177675943)
XLA Ops:
  0.6 6.1 %pack.1 = bf16[8448,128]{1,0:T(8,128)(2,1)} custom-call(s32[2,2]{1,0:T(2,128)} %bounds_hbm, s32[32]{0:T(128)} %lengths_hbm.1, bf16[4096,128]{1,0:T(8,128)(2,1)} %measures_hbm.1, s32[2,4096]{1,0:T(2,128)} %preds_hbm.1, s32[32,128]{1,0:T(8,128)} %bitcast.9, s32[32,128]{1,0:T(8,128)} %bitcast.10, s32[32,128]{1,0:T(8,128)} %bitcast.11), custom_call_target="tpu_custom_call" | custom-call | tf_op jit(solution)/shard_map/pack/pallas_call | solution.py:140
  6.7 0.0 copy-start
  6.8 42.4 %all_to_all.10 = bf16[128,33,2,128]{3,2,1,0:T(2,128)(2,1)S(1)} all-to-all(bf16[128,33,2,128]{3,2,1,0:T(2,128)(2,1)} %bitcast.8), channel_id=1, replica_groups=mesh['section'=4,'dom_0'=4,'dom_1'=4,'dom_2'=2] {'section','dom_0','dom_..., dimensions={0} | all-to-all | bytes 4325376 | tf_op jit(solution)/shard_map/all_to_all | solution.py:417
  49.2 0.0 copy-done
  49.2 9.9 %join.1 = (bf16[64,32,128]{2,1,0:T(8,128)(2,1)S(1)}, bf16[8192,256]{1,0:T(8,128)(2,1)S(1)}, f32[2,64,128]{2,1,0:T(8,128)S(1)}) custom-call(s32[1]{0:T(128)} %bitcast.me_ref, bf16[8448,128]{1,0:T(8,128)(2,1)S(1)} %bitcast.7, bf16[2048,128]{1,0:T(8,128)(2,1)S(1)} %copy-done), custom_call_target="tpu_custom_call" | custom-call | flops 9663676416 | bytes 8388608 | tf_op jit(solution)/shard_map/join/pallas_call | solution.py:251
  59.0 1.3 %collective-permute-start = (bf16[64,32,128]{2,1,0:T(8,128)(2,1)S(1)}, bf16[64,32,128]{2,1,0:T(8,128)(2,1)S(1)}, u32[]{:S(2)}, u32[]{:S(2)}) collective-permute-start(bf16[64,32,128]{2,1,0:T(8,128)(2,1)S(1)} %get-tuple-element.15), channel_id=1, source_target_pairs={{0,1},{1,0},{2,3},{3,2},{4,5},{5,4},{6,7},{7,6},{8,9},{9,8},{10,11... | collective-permute-start | bytes 1572872 | tf_op jit(solution)/shard_map/ppermute | solution.py:421
  60.4 4.5 %rest.1.own_ref = f32[64,32,128]{2,1,0:T(8,128)S(1)} custom-call(s32[1]{0:T(128)} %bitcast.me_ref, bf16[8192,256]{1,0:T(8,128)(2,1)S(1)} %get-tuple-element.13.pair_ref, f32[2,64,128]{2,1,0:T(8,128)S(1)} %get-tuple-element.14.group_ref), custom_call_target="tpu_custom_call" | custom-call | flops 5368709120 | bytes 8388608 | tf_op jit(solution)/shard_map/rest/pallas_call | solution.py:279
  64.9 0.0 collective-permute-done.got_ref
  64.9 0.3 merge.1
  65.1 19.1 %all_to_all.11.got_ref = bf16[64,48,128]{2,1,0:T(8,128)(2,1)S(1)} all-to-all(bf16[64,48,128]{2,1,0:T(8,128)(2,1)S(1)} %merge.1), channel_id=1, replica_groups=mesh['section'=4,'dom_0'=4,'dom_1'=4,'dom_2'=2] {'section','dom_0','dom_1'}, dimensions={0} | all-to-all | bytes 1572864 | tf_op jit(solution)/shard_map/all_to_all | solution.py:423
  84.2 0.1 total.1
  84.4 2.1 %collective-permute-start.1 = (f32[16,128]{1,0:T(8,128)S(1)}, f32[16,128]{1,0:T(8,128)S(1)}, u32[]{:S(2)}, u32[]{:S(2)}) collective-permute-start(f32[16,128]{1,0:T(8,128)S(1)} %get-tuple-element.17.a_ref), channel_id=1, source_target_pairs={{0,1},{1,0},{2,3},{3,2},{4,5},{5,4},{6,7},{7,6},{8,9},{9,8},{10,11... | collective-permute-start | bytes 24584 | tf_op jit(solution)/shard_map/ppermute | solution.py:425
  86.4 0.8 collective-permute-done.1.b_ref
  87.3 1.3 %leaders.1 = (f32[32,128]{1,0:T(8,128)}, f32[1,16]{1,0:T(1,128)}) custom-call(f32[32,128]{1,0:T(8,128)S(1)} %get-tuple-element.16.sums_ref, f32[16,128]{1,0:T(8,128)S(1)} %get-tuple-element.17.a_ref, f32[16,128]{1,0:T(8,128)S(1)} %collective-permute-done.1.b_ref), custom_call_target="tpu_custom_call" | custom-call | tf_op jit(solution)/shard_map/leaders/pallas_call | solution.py:384
Async XLA Ops:
  6.7 42.4 %copy-start = (bf16[2048,128]{1,0:T(8,128)(2,1)S(1)}, bf16[2048,128]{1,0:T(8,128)(2,1)}, u32[]{:S(2)}) copy-start(bf16[2048,128]{1,0:T(8,128)(2,1)} %table_ref.1) | copy-start | bytes 1572868
  59.0 5.8 %collective-permute-start = (bf16[64,32,128]{2,1,0:T(8,128)(2,1)S(1)}, bf16[64,32,128]{2,1,0:T(8,128)(2,1)S(1)}, u32[]{:S(2)}, u32[]{:S(2)}) collective-permute-start(bf16[64,32,128]{2,1,0:T(8,128)(2,1)S(1)} %get-tuple-element.15), channel_id=1, source_target_pairs={{0,1},{1,0},{2,3},{3,2},{4,5},{5,4},{6,7},{7,6},{8,9},{9,8},{10,11... | collective-permute-start | bytes 1572872 | tf_op jit(solution)/shard_map/ppermute | solution.py:421
  84.4 2.9 %collective-permute-start.1 = (f32[16,128]{1,0:T(8,128)S(1)}, f32[16,128]{1,0:T(8,128)S(1)}, u32[]{:S(2)}, u32[]{:S(2)}) collective-permute-start(f32[16,128]{1,0:T(8,128)S(1)} %get-tuple-element.17.a_ref), channel_id=1, source_target_pairs={{0,1},{1,0},{2,3},{3,2},{4,5},{5,4},{6,7},{7,6},{8,9},{9,8},{10,11... | collective-permute-start | bytes 24584 | tf_op jit(solution)/shard_map/ppermute | solution.py:425

commit v8 on v7

--- a/solution.py
+++ b/solution.py
@@ -355,11 +355,10 @@
     over = (down > best) | ((down == best) & (ids(square, 0) < ids(square, 1)))
     rank = jnp.sum(over.astype(F32), axis=0, keepdims=True).astype(I32)
     pick = (ids((TOPK, BLOCK), 0) == rank).astype(F32)
-    found = lax.dot_general(
-        pick, x, NT, precision=lax.Precision.HIGHEST, preferred_element_type=F32
+    copies = jnp.concatenate([x] * TOPK, axis=0)
+    tiled = lax.dot_general(
+        pick, copies, NT, precision=lax.Precision.HIGHEST, preferred_element_type=F32
     )
-    spread = (ids((x.shape[0], lanes), 0) == ids((x.shape[0], lanes), 1) % x.shape[0]).astype(F32)
-    tiled = jnp.dot(found, spread, precision=lax.Precision.HIGHEST, preferred_element_type=F32)
     keep = ids((TOPK, lanes), 0) == ids((TOPK, lanes), 1) // x.shape[0]
     flat = jnp.sum(jnp.where(keep, tiled, 0.0), axis=0, keepdims=True)
     pieces = [flat[:, n * BLOCK : (n + 1) * BLOCK] for n in range(4)]

time: 88.9 us -> 88.8 us (level)
  no operation moved by 1% of the time
where the time goes in v8:
time: 88.8 us; the launch traced here: 88.6 us
  blocking collectives  61.5 us (69%)
  Pallas kernels  22 us (25%)
  starting transfers between devices  3.41 us (4%)
    all_to_all x1, blocking collectives, on_device(): lax.all_to_all(packets.reshape(DESTS, AREA // 2, 2, BLOCK), DEVICES, spli...  42.4 us
    all_to_all x1, blocking collectives, on_device(): lax.all_to_all(pair, CHIPS, split_axis=0, concat_axis=0, tiled=True)  19.1 us
    pallas_call x1, Pallas kernels, join(): pl.pallas_call(join_kernel, out_shape=(jax.ShapeDtypeStruct((64, 32, BLOC...  9.87 us
    pallas_call x1, Pallas kernels, pack(): pl.pallas_call(pack_kernel, out_shape=jax.ShapeDtypeStruct((FLAT, BLOCK),...  6.1 us
    pallas_call x1, Pallas kernels, rest(): pl.pallas_call(rest_kernel, out_shape=jax.ShapeDtypeStruct((64, 32, BLOCK...  4.47 us
    ppermute x1, starting transfers between devices, on_device(): lax.ppermute(scores, CORE, SWAP)  2.08 us
  transfers between devices with their start and end apart: 2, of which 1 were waited for; matrix products, arithmetic and copies ran while one was open for 0% of the time, Pallas kernels for 5%

profile of v8, /device:TPU:1, one launch (start us, length us, event | category | flops | bytes accessed | tf_op | source)
XLA Modules:
  0.0 88.6 jit_solution(10342736430670972745)
XLA Ops:
  0.6 6.1 %pack.1 = bf16[8448,128]{1,0:T(8,128)(2,1)} custom-call(s32[2,2]{1,0:T(2,128)} %bounds_hbm, s32[32]{0:T(128)} %lengths_hbm.1, bf16[4096,128]{1,0:T(8,128)(2,1)} %measures_hbm.1, s32[2,4096]{1,0:T(2,128)} %preds_hbm.1, s32[32,128]{1,0:T(8,128)} %bitcast.9, s32[32,128]{1,0:T(8,128)} %bitcast.10, s32[32,128]{1,0:T(8,128)} %bitcast.11), custom_call_target="tpu_custom_call" | custom-call | tf_op jit(solution)/shard_map/pack/pallas_call | solution.py:140
  6.7 0.0 copy-start
  6.8 42.4 %all_to_all.10 = bf16[128,33,2,128]{3,2,1,0:T(2,128)(2,1)S(1)} all-to-all(bf16[128,33,2,128]{3,2,1,0:T(2,128)(2,1)} %bitcast.8), channel_id=1, replica_groups=mesh['section'=4,'dom_0'=4,'dom_1'=4,'dom_2'=2] {'section','dom_0','dom_..., dimensions={0} | all-to-all | bytes 4325376 | tf_op jit(solution)/shard_map/all_to_all | solution.py:416
  49.2 0.0 copy-done
  49.2 9.9 %join.1 = (bf16[64,32,128]{2,1,0:T(8,128)(2,1)S(1)}, bf16[8192,256]{1,0:T(8,128)(2,1)S(1)}, f32[2,64,128]{2,1,0:T(8,128)S(1)}) custom-call(s32[1]{0:T(128)} %bitcast.me_ref, bf16[8448,128]{1,0:T(8,128)(2,1)S(1)} %bitcast.7, bf16[2048,128]{1,0:T(8,128)(2,1)S(1)} %copy-done), custom_call_target="tpu_custom_call" | custom-call | flops 9663676416 | bytes 8388608 | tf_op jit(solution)/shard_map/join/pallas_call | solution.py:251
  59.0 1.3 %collective-permute-start = (bf16[64,32,128]{2,1,0:T(8,128)(2,1)S(1)}, bf16[64,32,128]{2,1,0:T(8,128)(2,1)S(1)}, u32[]{:S(2)}, u32[]{:S(2)}) collective-permute-start(bf16[64,32,128]{2,1,0:T(8,128)(2,1)S(1)} %get-tuple-element.15), channel_id=1, source_target_pairs={{0,1},{1,0},{2,3},{3,2},{4,5},{5,4},{6,7},{7,6},{8,9},{9,8},{10,11... | collective-permute-start | bytes 1572872 | tf_op jit(solution)/shard_map/ppermute | solution.py:420
  60.4 4.5 %rest.1.own_ref = f32[64,32,128]{2,1,0:T(8,128)S(1)} custom-call(s32[1]{0:T(128)} %bitcast.me_ref, bf16[8192,256]{1,0:T(8,128)(2,1)S(1)} %get-tuple-element.13.pair_ref, f32[2,64,128]{2,1,0:T(8,128)S(1)} %get-tuple-element.14.group_ref), custom_call_target="tpu_custom_call" | custom-call | flops 5368709120 | bytes 8388608 | tf_op jit(solution)/shard_map/rest/pallas_call | solution.py:279
  64.9 0.0 collective-permute-done.got_ref
  64.9 0.3 merge.1
  65.1 19.1 %all_to_all.11.got_ref = bf16[64,48,128]{2,1,0:T(8,128)(2,1)S(1)} all-to-all(bf16[64,48,128]{2,1,0:T(8,128)(2,1)S(1)} %merge.1), channel_id=1, replica_groups=mesh['section'=4,'dom_0'=4,'dom_1'=4,'dom_2'=2] {'section','dom_0','dom_1'}, dimensions={0} | all-to-all | bytes 1572864 | tf_op jit(solution)/shard_map/all_to_all | solution.py:422
  84.2 0.1 total.1
  84.4 2.1 %collective-permute-start.1 = (f32[16,128]{1,0:T(8,128)S(1)}, f32[16,128]{1,0:T(8,128)S(1)}, u32[]{:S(2)}, u32[]{:S(2)}) collective-permute-start(f32[16,128]{1,0:T(8,128)S(1)} %get-tuple-element.17.a_ref), channel_id=1, source_target_pairs={{0,1},{1,0},{2,3},{3,2},{4,5},{5,4},{6,7},{7,6},{8,9},{9,8},{10,11... | collective-permute-start | bytes 24584 | tf_op jit(solution)/shard_map/ppermute | solution.py:424
  86.4 0.8 collective-permute-done.1.b_ref
  87.3 1.1 %leaders.1 = (f32[32,128]{1,0:T(8,128)}, f32[1,16]{1,0:T(1,128)}) custom-call(f32[32,128]{1,0:T(8,128)S(1)} %get-tuple-element.16.sums_ref, f32[16,128]{1,0:T(8,128)S(1)} %get-tuple-element.17.a_ref, f32[16,128]{1,0:T(8,128)S(1)} %collective-permute-done.1.b_ref), custom_call_target="tpu_custom_call" | custom-call | tf_op jit(solution)/shard_map/leaders/pallas_call | solution.py:383
Async XLA Ops:
  6.7 42.4 %copy-start = (bf16[2048,128]{1,0:T(8,128)(2,1)S(1)}, bf16[2048,128]{1,0:T(8,128)(2,1)}, u32[]{:S(2)}) copy-start(bf16[2048,128]{1,0:T(8,128)(2,1)} %table_ref.1) | copy-start | bytes 1572868
  59.0 5.8 %collective-permute-start = (bf16[64,32,128]{2,1,0:T(8,128)(2,1)S(1)}, bf16[64,32,128]{2,1,0:T(8,128)(2,1)S(1)}, u32[]{:S(2)}, u32[]{:S(2)}) collective-permute-start(bf16[64,32,128]{2,1,0:T(8,128)(2,1)S(1)} %get-tuple-element.15), channel_id=1, source_target_pairs={{0,1},{1,0},{2,3},{3,2},{4,5},{5,4},{6,7},{7,6},{8,9},{9,8},{10,11... | collective-permute-start | bytes 1572872 | tf_op jit(solution)/shard_map/ppermute | solution.py:420
  84.4 2.9 %collective-permute-start.1 = (f32[16,128]{1,0:T(8,128)S(1)}, f32[16,128]{1,0:T(8,128)S(1)}, u32[]{:S(2)}, u32[]{:S(2)}) collective-permute-start(f32[16,128]{1,0:T(8,128)S(1)} %get-tuple-element.17.a_ref), channel_id=1, source_target_pairs={{0,1},{1,0},{2,3},{3,2},{4,5},{5,4},{6,7},{7,6},{8,9},{9,8},{10,11... | collective-permute-start | bytes 24584 | tf_op jit(solution)/shard_map/ppermute | solution.py:424

commit v9 on v8

--- a/solution.py
+++ b/solution.py
@@ -14,8 +14,8 @@
 FLAT = DESTS * AREA
 PIECES = 4
 PER = 8
-TILES = 2
-FETCH = 2
+TILES = 4
+FETCH = 4
 BF = jnp.bfloat16
 F32 = jnp.float32
 I32 = jnp.int32

time: 88.8 us -> 88.7 us (level)
  no operation moved by 1% of the time
where the time goes in v9:
time: 88.7 us; the launch traced here: 88.5 us
  blocking collectives  61.5 us (69%)
  Pallas kernels  21.9 us (25%)
  starting transfers between devices  3.41 us (4%)
    all_to_all x1, blocking collectives, on_device(): lax.all_to_all(packets.reshape(DESTS, AREA // 2, 2, BLOCK), DEVICES, spli...  42.4 us
    all_to_all x1, blocking collectives, on_device(): lax.all_to_all(pair, CHIPS, split_axis=0, concat_axis=0, tiled=True)  19.1 us
    pallas_call x1, Pallas kernels, join(): pl.pallas_call(join_kernel, out_shape=(jax.ShapeDtypeStruct((64, 32, BLOC...  9.76 us
    pallas_call x1, Pallas kernels, pack(): pl.pallas_call(pack_kernel, out_shape=jax.ShapeDtypeStruct((FLAT, BLOCK),...  6.1 us
    pallas_call x1, Pallas kernels, rest(): pl.pallas_call(rest_kernel, out_shape=jax.ShapeDtypeStruct((64, 32, BLOCK...  4.48 us
    ppermute x1, starting transfers between devices, on_device(): lax.ppermute(scores, CORE, SWAP)  2.08 us
  transfers between devices with their start and end apart: 2, of which 1 were waited for; matrix products, arithmetic and copies ran while one was open for 0% of the time, Pallas kernels for 5%

profile of v9, /device:TPU:1, one launch (start us, length us, event | category | flops | bytes accessed | tf_op | source)
XLA Modules:
  0.0 88.5 jit_solution(18317059471373475658)
XLA Ops:
  0.6 6.1 %pack.1 = bf16[8448,128]{1,0:T(8,128)(2,1)} custom-call(s32[2,2]{1,0:T(2,128)} %bounds_hbm, s32[32]{0:T(128)} %lengths_hbm.1, bf16[4096,128]{1,0:T(8,128)(2,1)} %measures_hbm.1, s32[2,4096]{1,0:T(2,128)} %preds_hbm.1, s32[32,128]{1,0:T(8,128)} %bitcast.9, s32[32,128]{1,0:T(8,128)} %bitcast.10, s32[32,128]{1,0:T(8,128)} %bitcast.11), custom_call_target="tpu_custom_call" | custom-call | tf_op jit(solution)/shard_map/pack/pallas_call | solution.py:140
  6.7 0.0 copy-start
  6.8 42.4 %all_to_all.10 = bf16[128,33,2,128]{3,2,1,0:T(2,128)(2,1)S(1)} all-to-all(bf16[128,33,2,128]{3,2,1,0:T(2,128)(2,1)} %bitcast.8), channel_id=1, replica_groups=mesh['section'=4,'dom_0'=4,'dom_1'=4,'dom_2'=2] {'section','dom_0','dom_..., dimensions={0} | all-to-all | bytes 4325376 | tf_op jit(solution)/shard_map/all_to_all | solution.py:416
  49.2 0.0 copy-done
  49.2 9.8 %join.1 = (bf16[64,32,128]{2,1,0:T(8,128)(2,1)S(1)}, bf16[8192,256]{1,0:T(8,128)(2,1)S(1)}, f32[2,64,128]{2,1,0:T(8,128)S(1)}) custom-call(s32[1]{0:T(128)} %bitcast.me_ref, bf16[8448,128]{1,0:T(8,128)(2,1)S(1)} %bitcast.7, bf16[2048,128]{1,0:T(8,128)(2,1)S(1)} %copy-done), custom_call_target="tpu_custom_call" | custom-call | flops 9663676416 | bytes 8388608 | tf_op jit(solution)/shard_map/join/pallas_call | solution.py:251
  58.9 1.3 %collective-permute-start = (bf16[64,32,128]{2,1,0:T(8,128)(2,1)S(1)}, bf16[64,32,128]{2,1,0:T(8,128)(2,1)S(1)}, u32[]{:S(2)}, u32[]{:S(2)}) collective-permute-start(bf16[64,32,128]{2,1,0:T(8,128)(2,1)S(1)} %get-tuple-element.15), channel_id=1, source_target_pairs={{0,1},{1,0},{2,3},{3,2},{4,5},{5,4},{6,7},{7,6},{8,9},{9,8},{10,11... | collective-permute-start | bytes 1572872 | tf_op jit(solution)/shard_map/ppermute | solution.py:420
  60.3 4.5 %rest.1.own_ref = f32[64,32,128]{2,1,0:T(8,128)S(1)} custom-call(s32[1]{0:T(128)} %bitcast.me_ref, bf16[8192,256]{1,0:T(8,128)(2,1)S(1)} %get-tuple-element.13.pair_ref, f32[2,64,128]{2,1,0:T(8,128)S(1)} %get-tuple-element.14.group_ref), custom_call_target="tpu_custom_call" | custom-call | flops 5368709120 | bytes 8388608 | tf_op jit(solution)/shard_map/rest/pallas_call | solution.py:279
  64.8 0.0 collective-permute-done.got_ref
  64.8 0.3 merge.1
  65.0 19.1 %all_to_all.11.got_ref = bf16[64,48,128]{2,1,0:T(8,128)(2,1)S(1)} all-to-all(bf16[64,48,128]{2,1,0:T(8,128)(2,1)S(1)} %merge.1), channel_id=1, replica_groups=mesh['section'=4,'dom_0'=4,'dom_1'=4,'dom_2'=2] {'section','dom_0','dom_1'}, dimensions={0} | all-to-all | bytes 1572864 | tf_op jit(solution)/shard_map/all_to_all | solution.py:422
  84.1 0.1 total.1
  84.3 2.1 %collective-permute-start.1 = (f32[16,128]{1,0:T(8,128)S(1)}, f32[16,128]{1,0:T(8,128)S(1)}, u32[]{:S(2)}, u32[]{:S(2)}) collective-permute-start(f32[16,128]{1,0:T(8,128)S(1)} %get-tuple-element.17.a_ref), channel_id=1, source_target_pairs={{0,1},{1,0},{2,3},{3,2},{4,5},{5,4},{6,7},{7,6},{8,9},{9,8},{10,11... | collective-permute-start | bytes 24584 | tf_op jit(solution)/shard_map/ppermute | solution.py:424
  86.3 0.8 collective-permute-done.1.b_ref
  87.2 1.1 %leaders.1 = (f32[32,128]{1,0:T(8,128)}, f32[1,16]{1,0:T(1,128)}) custom-call(f32[32,128]{1,0:T(8,128)S(1)} %get-tuple-element.16.sums_ref, f32[16,128]{1,0:T(8,128)S(1)} %get-tuple-element.17.a_ref, f32[16,128]{1,0:T(8,128)S(1)} %collective-permute-done.1.b_ref), custom_call_target="tpu_custom_call" | custom-call | tf_op jit(solution)/shard_map/leaders/pallas_call | solution.py:383
Async XLA Ops:
  6.7 42.4 %copy-start = (bf16[2048,128]{1,0:T(8,128)(2,1)S(1)}, bf16[2048,128]{1,0:T(8,128)(2,1)}, u32[]{:S(2)}) copy-start(bf16[2048,128]{1,0:T(8,128)(2,1)} %table_ref.1) | copy-start | bytes 1572868
  58.9 5.8 %collective-permute-start = (bf16[64,32,128]{2,1,0:T(8,128)(2,1)S(1)}, bf16[64,32,128]{2,1,0:T(8,128)(2,1)S(1)}, u32[]{:S(2)}, u32[]{:S(2)}) collective-permute-start(bf16[64,32,128]{2,1,0:T(8,128)(2,1)S(1)} %get-tuple-element.15), channel_id=1, source_target_pairs={{0,1},{1,0},{2,3},{3,2},{4,5},{5,4},{6,7},{7,6},{8,9},{9,8},{10,11... | collective-permute-start | bytes 1572872 | tf_op jit(solution)/shard_map/ppermute | solution.py:420
  84.3 2.9 %collective-permute-start.1 = (f32[16,128]{1,0:T(8,128)S(1)}, f32[16,128]{1,0:T(8,128)S(1)}, u32[]{:S(2)}, u32[]{:S(2)}) collective-permute-start(f32[16,128]{1,0:T(8,128)S(1)} %get-tuple-element.17.a_ref), channel_id=1, source_target_pairs={{0,1},{1,0},{2,3},{3,2},{4,5},{5,4},{6,7},{7,6},{8,9},{9,8},{10,11... | collective-permute-start | bytes 24584 | tf_op jit(solution)/shard_map/ppermute | solution.py:424
